TPU v7x, 32 devices: a 4x4x1 block of a 4x4x8 slice. The times are simulated.
32 devices in a mesh: data: 1 (over z), dap2: 4 (over y), dap: 8 (over x, core).
Axes of the slice: x: 4, y: 4, z: 1, core: 2. Of those that a mesh axis runs over, the one named last changes fastest.
The devices are a block of a 4x4x8 slice.
Arguments:
- pair_rep: bfloat16 [1024, 1024, 128], P(('data', 'dap2', 'dap'))
- pair_mask: int32 [1024, 1024], P(('data', 'dap2', 'dap'))
- norm_in: bfloat16 [3, 2, 2, 128], replicated
- norm_out: bfloat16 [3, 2, 2, 128], replicated
- w_ab: bfloat16 [3, 2, 128, 512], replicated
- w_gate: bfloat16 [3, 2, 128, 128], replicated
- w_out: bfloat16 [3, 2, 128, 128], replicated
Outputs:
- output: bfloat16 [1024, 1024, 128], P(('data', 'dap2', 'dap'))
All inputs are finite; a program needn't handle non-finite values.
Results may differ from a plain program's by a relative error of at most 0.00996528.
Values are sent between devices in bfloat16 or wider.
A program may use at most 768 MiB of HBM per device.

v0:
```python
import jax
import jax.numpy as jnp
from jax import lax
from jax.sharding import PartitionSpec as P

LN_EPS = 1e-5
ROW_AXES = ("dap2", "dap")
ALL_ROWS = ("data", "dap2", "dap")


def layer_norm(values, gain_vec, shift_vec, norm_axis):
    mean_val = jnp.mean(values, axis=norm_axis, keepdims=True)
    centered = values - mean_val
    var_val = jnp.mean(centered * centered, axis=norm_axis, keepdims=True)
    return centered * lax.rsqrt(var_val + LN_EPS) * gain_vec + shift_vec


def row_inputs(pair_loc, mask_loc, norm_in, w_ab):
    hidden = w_ab.shape[1] // 4
    pair_f = pair_loc.astype(jnp.float32)
    x_ln = layer_norm(pair_f, norm_in[0].astype(jnp.float32), norm_in[1].astype(jnp.float32), -1).astype(jnp.bfloat16)
    proj_all = jnp.einsum("de,ikd->eik", w_ab, x_ln, preferred_element_type=jnp.float32)
    proj_four = proj_all.reshape(2, 2, hidden, pair_loc.shape[0], pair_loc.shape[1])
    ab_rows = (mask_loc * jax.nn.sigmoid(proj_four[:, 1]) * proj_four[:, 0]).astype(jnp.bfloat16)
    return pair_f, x_ln, ab_rows


def finish_update(pair_f, x_ln, tri_rows, norm_out, w_gate, w_out):
    gain_vec = norm_out[0].astype(jnp.float32)[:, None, None]
    shift_vec = norm_out[1].astype(jnp.float32)[:, None, None]
    y_ln = layer_norm(tri_rows.astype(jnp.float32), gain_vec, shift_vec, 0).astype(jnp.bfloat16)
    update_val = jnp.einsum("cij,cd->ijd", y_ln, w_out, preferred_element_type=jnp.float32)
    gate_val = jax.nn.sigmoid(jnp.einsum("ijd,de->ije", x_ln, w_gate, preferred_element_type=jnp.float32))
    return (pair_f + gate_val * update_val).astype(jnp.bfloat16)


def tri_update(pair_loc, mask_loc, norm_in, norm_out, w_ab, w_gate, w_out, outgoing):
    pair_f, x_ln, ab_rows = row_inputs(pair_loc, mask_loc, norm_in, w_ab)
    ab_cols = lax.all_to_all(ab_rows, ROW_AXES, 1, 2, tiled=True)
    einsum_form = "cik,cjk->cij" if outgoing else "cki,ckj->cij"
    tri_full = jnp.einsum(einsum_form, ab_cols[0], ab_cols[1], preferred_element_type=jnp.float32).astype(jnp.bfloat16)
    tri_rows = lax.all_to_all(tri_full, ROW_AXES, 1, 0, tiled=True)
    return finish_update(pair_f, x_ln, tri_rows, norm_out, w_gate, w_out)


def solution(mesh):
    row_spec = P(ALL_ROWS, None, None)
    mask_spec = P(ALL_ROWS, None)

    def local_stack(pair_rep, pair_mask, norm_in, norm_out, w_ab, w_gate, w_out):
        mask_f = pair_mask.astype(jnp.float32)
        pair_cur = pair_rep
        for layer_idx in range(w_ab.shape[0]):
            for upd_idx in range(2):
                pair_cur = tri_update(pair_cur, mask_f, norm_in[layer_idx, upd_idx], norm_out[layer_idx, upd_idx], w_ab[layer_idx, upd_idx], w_gate[layer_idx, upd_idx], w_out[layer_idx, upd_idx], upd_idx == 0)
        return pair_cur

    return jax.shard_map(local_stack, mesh=mesh, in_specs=(row_spec, mask_spec, P(), P(), P(), P(), P()), out_specs=row_spec, check_vma=False)
```

profile of v0, /device:TPU:103, one launch (start us, length us, event | category | flops | bytes accessed | tf_op | source)
XLA Modules:
  0.0 3480.2 jit_solution(13114369157047436753)
XLA Ops:
  0.0 11.9 copy.288
  24.2 27.0 fusion.143
  51.2 43.6 %fusion.198 = (f32[2,1,128,32,1024]{4,2,1,0,3:T(8,128)}, f32[2,1,128,32,1024]{4,2,1,0,3:T(8,128)}) fusion(f32[2,2,128,32,1024]{4,2,1,0,3:T(8,128)} %bitcast.7), kind=kLoop, calls=%fused_computation.279 | loop fusion | bytes 134217728 | tf_op jit(solution)/shard_map/slice | solution.py:24
  95.5 60.5 %fusion.36 = bf16[2,128,32,1024]{3,2,0,1:T(8,128)(2,1)} fusion(f32[2,1,128,32,1024]{4,2,1,0,3:T(8,128)} %get-tuple-element.28, f32[2,1,128,32,1024]{4,2,1,0,3:T(8,128)} %get-tuple-element.27, f32[32,1024]{1,0:T(8,128)S(1)} %convert_element_type.447), kind=kLoop, calls=%fused_computation.47 | loop fusion | flops 50331648 | bytes 84017152 | tf_op jit(solution)/shard_map/convert_element_type | solution.py:24
  156.0 209.9 %all_to_all.144 = bf16[2,128,32,1024]{3,2,0,1:T(8,128)(2,1)S(1)} all-to-all(bf16[2,128,32,1024]{3,2,0,1:T(8,128)(2,1)} %fusion.36), channel_id=1, replica_groups=mesh['data'=1,'dap2'=4,'dap'=8] {'dap2','dap'}, dimensions={1} | all-to-all | bytes 33554432 | tf_op jit(solution)/shard_map/all_to_all | solution.py:39
  374.5 15.7 convolution_convert_fusion.5
  390.2 12.2 copy.296
  410.6 13.0 fusion.164
  423.5 98.9 %all-to-all-done.1 = bf16[4,1024,1024]{2,0,1:T(4,128)(2,1)} async-done(((bf16[4,1024,1024]{2,0,1:T(4,128)(2,1)}), bf16[4,1024,1024]{2,0,1:T(4,128)(2,1)}, u32[]{:S(2)}, u32[]{:S(2)}) %all-to-all-start.1) | async-done | bytes 8388640 | tf_op jit(solution)/shard_map/all_to_all | solution.py:42
  553.3 12.5 convert_element_type.458
  565.9 16.8 convert_reduce_fusion.4
  588.8 27.0 fusion.141
  615.8 43.8 %fusion.197 = (f32[2,1,128,32,1024]{4,2,1,0,3:T(8,128)}, f32[2,1,128,32,1024]{4,2,1,0,3:T(8,128)}) fusion(f32[2,2,128,32,1024]{4,2,1,0,3:T(8,128)} %bitcast.27), kind=kLoop, calls=%fused_computation.278 | loop fusion | bytes 134217728 | tf_op jit(solution)/shard_map/slice | solution.py:24
  659.5 60.3 %fusion.29 = bf16[2,128,32,1024]{3,2,0,1:T(8,128)(2,1)} fusion(f32[2,1,128,32,1024]{4,2,1,0,3:T(8,128)} %get-tuple-element.26, f32[2,1,128,32,1024]{4,2,1,0,3:T(8,128)} %get-tuple-element.25, f32[32,1024]{1,0:T(8,128)S(1)} %copy-done.1), kind=kLoop, calls=%fused_computation.38 | loop fusion | flops 50331648 | bytes 84017152 | tf_op jit(solution)/shard_map/convert_element_type | solution.py:24
  719.9 199.2 %all_to_all.145 = bf16[2,128,32,1024]{3,2,0,1:T(8,128)(2,1)S(1)} all-to-all(bf16[2,128,32,1024]{3,2,0,1:T(8,128)(2,1)} %fusion.29), channel_id=1, replica_groups=mesh['data'=1,'dap2'=4,'dap'=8] {'dap2','dap'}, dimensions={1} | all-to-all | bytes 33554432 | tf_op jit(solution)/shard_map/all_to_all | solution.py:39
  944.6 13.7 convolution_convert_fusion.4
  958.3 22.8 copy.309
  981.1 17.5 all-to-all-start.3
  998.8 13.0 fusion.161
  1011.8 100.0 %all-to-all-done.3 = bf16[4,1024,1024]{2,0,1:T(4,128)(2,1)} async-done(((bf16[4,1024,1024]{2,0,1:T(4,128)(2,1)}), bf16[4,1024,1024]{2,0,1:T(4,128)(2,1)}, u32[]{:S(2)}, u32[]{:S(2)}) %all-to-all-start.3) | async-done | bytes 8388640 | tf_op jit(solution)/shard_map/all_to_all | solution.py:42
  1142.8 12.5 convert_element_type.476
  1155.4 16.8 convert_reduce_fusion.3
  1178.4 27.0 fusion.139
  1205.3 43.8 %fusion.196 = (f32[2,1,128,32,1024]{4,2,1,0,3:T(8,128)}, f32[2,1,128,32,1024]{4,2,1,0,3:T(8,128)}) fusion(f32[2,2,128,32,1024]{4,2,1,0,3:T(8,128)} %bitcast.48), kind=kLoop, calls=%fused_computation.277 | loop fusion | bytes 134217728 | tf_op jit(solution)/shard_map/slice | solution.py:24
  1249.1 60.3 %fusion.22 = bf16[2,128,32,1024]{3,2,0,1:T(8,128)(2,1)} fusion(f32[2,1,128,32,1024]{4,2,1,0,3:T(8,128)} %get-tuple-element.24, f32[2,1,128,32,1024]{4,2,1,0,3:T(8,128)} %get-tuple-element.23, f32[32,1024]{1,0:T(8,128)S(1)} %copy-done.2), kind=kLoop, calls=%fused_computation.29 | loop fusion | flops 50331648 | bytes 84017152 | tf_op jit(solution)/shard_map/convert_element_type | solution.py:24
  1309.4 205.2 %all_to_all.146 = bf16[2,128,32,1024]{3,2,0,1:T(8,128)(2,1)S(1)} all-to-all(bf16[2,128,32,1024]{3,2,0,1:T(8,128)(2,1)} %fusion.22), channel_id=1, replica_groups=mesh['data'=1,'dap2'=4,'dap'=8] {'dap2','dap'}, dimensions={1} | all-to-all | bytes 33554432 | tf_op jit(solution)/shard_map/all_to_all | solution.py:39
  1523.3 15.7 convolution_convert_fusion.3
  1539.0 12.1 copy.319
  1558.7 13.0 fusion.158
  1571.7 99.5 %all-to-all-done.5 = bf16[4,1024,1024]{2,0,1:T(4,128)(2,1)} async-done(((bf16[4,1024,1024]{2,0,1:T(4,128)(2,1)}), bf16[4,1024,1024]{2,0,1:T(4,128)(2,1)}, u32[]{:S(2)}, u32[]{:S(2)}) %all-to-all-start.5) | async-done | bytes 8388640 | tf_op jit(solution)/shard_map/all_to_all | solution.py:42
  1702.1 12.5 convert_element_type.494
  1714.6 16.8 convert_reduce_fusion.2
  1737.6 27.0 fusion.137
  1764.6 43.8 %fusion.195 = (f32[2,1,128,32,1024]{4,2,1,0,3:T(8,128)}, f32[2,1,128,32,1024]{4,2,1,0,3:T(8,128)}) fusion(f32[2,2,128,32,1024]{4,2,1,0,3:T(8,128)} %bitcast.68), kind=kLoop, calls=%fused_computation.276 | loop fusion | bytes 134217728 | tf_op jit(solution)/shard_map/slice | solution.py:24
  1808.4 60.3 %fusion.15 = bf16[2,128,32,1024]{3,2,0,1:T(8,128)(2,1)} fusion(f32[2,1,128,32,1024]{4,2,1,0,3:T(8,128)} %get-tuple-element.22, f32[2,1,128,32,1024]{4,2,1,0,3:T(8,128)} %get-tuple-element.21, f32[32,1024]{1,0:T(8,128)S(1)} %copy-done.3), kind=kLoop, calls=%fused_computation.20 | loop fusion | flops 50331648 | bytes 84017152 | tf_op jit(solution)/shard_map/convert_element_type | solution.py:24
  1868.7 199.2 %all_to_all.147 = bf16[2,128,32,1024]{3,2,0,1:T(8,128)(2,1)S(1)} all-to-all(bf16[2,128,32,1024]{3,2,0,1:T(8,128)(2,1)} %fusion.15), channel_id=1, replica_groups=mesh['data'=1,'dap2'=4,'dap'=8] {'dap2','dap'}, dimensions={1} | all-to-all | bytes 33554432 | tf_op jit(solution)/shard_map/all_to_all | solution.py:39
  2093.4 13.7 convolution_convert_fusion.2
  2107.2 22.8 copy.332
  2129.9 17.5 all-to-all-start.7
  2147.6 13.0 fusion.155
  2160.6 100.0 %all-to-all-done.7 = bf16[4,1024,1024]{2,0,1:T(4,128)(2,1)} async-done(((bf16[4,1024,1024]{2,0,1:T(4,128)(2,1)}), bf16[4,1024,1024]{2,0,1:T(4,128)(2,1)}, u32[]{:S(2)}, u32[]{:S(2)}) %all-to-all-start.7) | async-done | bytes 8388640 | tf_op jit(solution)/shard_map/all_to_all | solution.py:42
  2291.7 12.5 convert_element_type.512
  2304.2 16.8 convert_reduce_fusion.1
  2327.1 27.0 fusion.135
  2354.1 43.8 %fusion.194 = (f32[2,1,128,32,1024]{4,2,1,0,3:T(8,128)}, f32[2,1,128,32,1024]{4,2,1,0,3:T(8,128)}) fusion(f32[2,2,128,32,1024]{4,2,1,0,3:T(8,128)} %bitcast.89), kind=kLoop, calls=%fused_computation.275 | loop fusion | bytes 134217728 | tf_op jit(solution)/shard_map/slice | solution.py:24
  2397.9 60.3 %fusion.8 = bf16[2,128,32,1024]{3,2,0,1:T(8,128)(2,1)} fusion(f32[2,1,128,32,1024]{4,2,1,0,3:T(8,128)} %get-tuple-element.20, f32[2,1,128,32,1024]{4,2,1,0,3:T(8,128)} %get-tuple-element.19, f32[32,1024]{1,0:T(8,128)S(1)} %copy-done.4), kind=kLoop, calls=%fused_computation.11 | loop fusion | flops 50331648 | bytes 84017152 | tf_op jit(solution)/shard_map/convert_element_type | solution.py:24
  2458.2 205.2 %all_to_all.148 = bf16[2,128,32,1024]{3,2,0,1:T(8,128)(2,1)S(1)} all-to-all(bf16[2,128,32,1024]{3,2,0,1:T(8,128)(2,1)} %fusion.8), channel_id=1, replica_groups=mesh['data'=1,'dap2'=4,'dap'=8] {'dap2','dap'}, dimensions={1} | all-to-all | bytes 33554432 | tf_op jit(solution)/shard_map/all_to_all | solution.py:39
  2672.0 15.7 convolution_convert_fusion.1
  2687.8 12.1 copy.342
  2707.5 13.0 fusion.152
  2720.4 99.6 %all-to-all-done.9 = bf16[4,1024,1024]{2,0,1:T(4,128)(2,1)} async-done(((bf16[4,1024,1024]{2,0,1:T(4,128)(2,1)}), bf16[4,1024,1024]{2,0,1:T(4,128)(2,1)}, u32[]{:S(2)}, u32[]{:S(2)}) %all-to-all-start.9) | async-done | bytes 8388640 | tf_op jit(solution)/shard_map/all_to_all | solution.py:42
  2850.9 12.5 convert_element_type.530
  2863.4 16.8 convert_reduce_fusion
  2886.4 27.0 fusion.133
  2913.4 43.8 %fusion.193 = (f32[2,1,128,32,1024]{4,2,1,0,3:T(8,128)}, f32[2,1,128,32,1024]{4,2,1,0,3:T(8,128)}) fusion(f32[2,2,128,32,1024]{4,2,1,0,3:T(8,128)} %bitcast.109), kind=kLoop, calls=%fused_computation.274 | loop fusion | bytes 134217728 | tf_op jit(solution)/shard_map/slice | solution.py:24
  2957.2 60.3 %fusion.1 = bf16[2,128,32,1024]{3,2,0,1:T(8,128)(2,1)} fusion(f32[2,1,128,32,1024]{4,2,1,0,3:T(8,128)} %get-tuple-element.18, f32[2,1,128,32,1024]{4,2,1,0,3:T(8,128)} %get-tuple-element.17, f32[32,1024]{1,0:T(8,128)S(1)} %copy-done.5), kind=kLoop, calls=%fused_computation.2 | loop fusion | flops 50331648 | bytes 84017152 | tf_op jit(solution)/shard_map/convert_element_type | solution.py:24
  3017.5 199.2 %all_to_all.149 = bf16[2,128,32,1024]{3,2,0,1:T(8,128)(2,1)S(1)} all-to-all(bf16[2,128,32,1024]{3,2,0,1:T(8,128)(2,1)} %fusion.1), channel_id=1, replica_groups=mesh['data'=1,'dap2'=4,'dap'=8] {'dap2','dap'}, dimensions={1} | all-to-all | bytes 33554432 | tf_op jit(solution)/shard_map/all_to_all | solution.py:39
  3242.2 13.8 convolution_convert_fusion
  3255.9 22.8 copy.355
  3278.7 17.9 all-to-all-start.11
  3297.0 13.3 fusion.167
  3310.3 100.2 %all-to-all-done.11 = bf16[4,1024,1024]{2,0,1:T(4,128)(2,1)} async-done(((bf16[4,1024,1024]{2,0,1:T(4,128)(2,1)}), bf16[4,1024,1024]{2,0,1:T(4,128)(2,1)}, u32[]{:S(2)}, u32[]{:S(2)}) %all-to-all-start.11) | async-done | bytes 8388640 | tf_op jit(solution)/shard_map/all_to_all | solution.py:42
  3449.1 18.9 fusion.83
  3468.1 11.9 copy.362
  (152 shorter events, 363.4 us)
Async XLA Ops:
  0.0 11.9 copy-start.7
  51.2 43.6 %copy-start.6 = (s32[32,1024]{1,0:T(8,128)S(1)}, s32[32,1024]{1,0:T(8,128)}, u32[]{:S(2)}) copy-start(s32[32,1024]{1,0:T(8,128)} %param.8) | copy-start | bytes 393220
  94.8 0.6 copy-start
  390.2 19.5 copy-start.8
  402.4 120.1 %all-to-all-start.1 = ((bf16[4,1024,1024]{2,0,1:T(4,128)(2,1)}), bf16[4,1024,1024]{2,0,1:T(4,128)(2,1)}, u32[]{:S(2)}, u32[]{:S(2)}) async-start(bf16[4,1024,1024]{2,0,1:T(4,128)(2,1)} %copy.296), calls=%async_computation.1 | async-start | bytes 16777216 | tf_op jit(solution)/shard_map/all_to_all | solution.py:42
  565.9 22.9 copy-start.17
  565.9 22.9 copy-start.18
  615.7 43.8 %copy-start.1 = (f32[32,1024]{1,0:T(8,128)S(1)}, f32[32,1024]{1,0:T(8,128)}, u32[]{:S(2)}) copy-start(f32[32,1024]{1,0:T(8,128)} %copy-done) | copy-start | bytes 393220
  958.3 40.3 %copy-start.28 = (f32[128]{0:T(128)S(1)}, f32[128]{0:T(128)}, u32[]{:S(2)}) copy-start(f32[128]{0:T(128)} %get-tuple-element.12) | copy-start | bytes 1540
  958.3 40.4 %copy-start.27 = (f32[128]{0:T(128)S(1)}, f32[128]{0:T(128)}, u32[]{:S(2)}) copy-start(f32[128]{0:T(128)} %get-tuple-element.13) | copy-start | bytes 1540
  981.1 130.6 %all-to-all-start.3 = ((bf16[4,1024,1024]{2,0,1:T(4,128)(2,1)}), bf16[4,1024,1024]{2,0,1:T(4,128)(2,1)}, u32[]{:S(2)}, u32[]{:S(2)}) async-start(bf16[4,1024,1024]{2,0,1:T(4,128)(2,1)} %copy.309), calls=%async_computation.3 | async-start | bytes 16777216 | tf_op jit(solution)/shard_map/all_to_all | solution.py:42
  1155.4 23.0 copy-start.15
  1155.4 23.0 copy-start.16
  1205.3 43.8 %copy-start.2 = (f32[32,1024]{1,0:T(8,128)S(1)}, f32[32,1024]{1,0:T(8,128)}, u32[]{:S(2)}) copy-start(f32[32,1024]{1,0:T(8,128)} %copy-done) | copy-start | bytes 393220
  1539.0 19.5 copy-start.26
  1539.0 19.6 copy-start.25
  1551.1 120.1 %all-to-all-start.5 = ((bf16[4,1024,1024]{2,0,1:T(4,128)(2,1)}), bf16[4,1024,1024]{2,0,1:T(4,128)(2,1)}, u32[]{:S(2)}, u32[]{:S(2)}) async-start(bf16[4,1024,1024]{2,0,1:T(4,128)(2,1)} %copy.319), calls=%async_computation.5 | async-start | bytes 16777216 | tf_op jit(solution)/shard_map/all_to_all | solution.py:42
  1714.6 23.0 copy-start.13
  1714.6 23.0 copy-start.14
  1764.6 43.8 %copy-start.3 = (f32[32,1024]{1,0:T(8,128)S(1)}, f32[32,1024]{1,0:T(8,128)}, u32[]{:S(2)}) copy-start(f32[32,1024]{1,0:T(8,128)} %copy-done) | copy-start | bytes 393220
  2107.1 40.3 %copy-start.24 = (f32[128]{0:T(128)S(1)}, f32[128]{0:T(128)}, u32[]{:S(2)}) copy-start(f32[128]{0:T(128)} %get-tuple-element.8) | copy-start | bytes 1540
  2107.1 40.4 %copy-start.23 = (f32[128]{0:T(128)S(1)}, f32[128]{0:T(128)}, u32[]{:S(2)}) copy-start(f32[128]{0:T(128)} %get-tuple-element.9) | copy-start | bytes 1540
  2129.9 130.6 %all-to-all-start.7 = ((bf16[4,1024,1024]{2,0,1:T(4,128)(2,1)}), bf16[4,1024,1024]{2,0,1:T(4,128)(2,1)}, u32[]{:S(2)}, u32[]{:S(2)}) async-start(bf16[4,1024,1024]{2,0,1:T(4,128)(2,1)} %copy.332), calls=%async_computation.7 | async-start | bytes 16777216 | tf_op jit(solution)/shard_map/all_to_all | solution.py:42
  2304.2 22.9 copy-start.11
  2304.2 22.9 copy-start.12
  2354.1 43.8 %copy-start.4 = (f32[32,1024]{1,0:T(8,128)S(1)}, f32[32,1024]{1,0:T(8,128)}, u32[]{:S(2)}) copy-start(f32[32,1024]{1,0:T(8,128)} %copy-done) | copy-start | bytes 393220
  2687.8 19.5 copy-start.22
  2687.8 19.6 copy-start.21
  2699.9 120.1 %all-to-all-start.9 = ((bf16[4,1024,1024]{2,0,1:T(4,128)(2,1)}), bf16[4,1024,1024]{2,0,1:T(4,128)(2,1)}, u32[]{:S(2)}, u32[]{:S(2)}) async-start(bf16[4,1024,1024]{2,0,1:T(4,128)(2,1)} %copy.342), calls=%async_computation.9 | async-start | bytes 16777216 | tf_op jit(solution)/shard_map/all_to_all | solution.py:42
  2863.4 23.0 copy-start.9
  2863.4 23.0 copy-start.10
  2913.4 43.8 %copy-start.5 = (f32[32,1024]{1,0:T(8,128)S(1)}, f32[32,1024]{1,0:T(8,128)}, u32[]{:S(2)}) copy-start(f32[32,1024]{1,0:T(8,128)} %copy-done) | copy-start | bytes 393220
  3255.9 40.7 %copy-start.20 = (f32[128]{0:T(128)S(1)}, f32[128]{0:T(128)}, u32[]{:S(2)}) copy-start(f32[128]{0:T(128)} %get-tuple-element.16) | copy-start | bytes 1540
  3255.9 40.9 %copy-start.19 = (f32[128]{0:T(128)S(1)}, f32[128]{0:T(128)}, u32[]{:S(2)}) copy-start(f32[128]{0:T(128)} %get-tuple-element.5) | copy-start | bytes 1540
  3278.7 131.8 %all-to-all-start.11 = ((bf16[4,1024,1024]{2,0,1:T(4,128)(2,1)}), bf16[4,1024,1024]{2,0,1:T(4,128)(2,1)}, u32[]{:S(2)}, u32[]{:S(2)}) async-start(bf16[4,1024,1024]{2,0,1:T(4,128)(2,1)} %copy.355), calls=%async_computation.11 | async-start | bytes 16777216 | tf_op jit(solution)/shard_map/all_to_all | solution.py:42
where the time goes:
time: 3490 us; the launch traced here: 3480 us
  blocking collectives  1220 us (35%)
  local copies, waits for them, and re-layouts  607 us (17%)
  waiting for transfers between devices  598 us (17%)
  other arithmetic  551 us (16%)
  matrix products  431 us (12%)
  starting transfers between devices  74.7 us (2%)
    all_to_all x6, blocking collectives, tri_update(): ab_cols = lax.all_to_all(ab_rows, ROW_AXES, 1, 2, tiled=True)  1220 us
    all_to_all x6, waiting for transfers between devices, tri_update(): tri_rows = lax.all_to_all(tri_full, ROW_AXES, 1, 0, tiled=True)  598 us
    convert_element_type x6, other arithmetic, row_inputs(): (mask_loc * jax.nn.sigmoid(proj_four[:, 1]) * proj_four[:, 0]).astype(jnp...  362 us
    slice x6, local copies, waits for them, and re-layouts, row_inputs(): proj_four[:, 1]  263 us
    dot_general x6, matrix products, row_inputs(): jnp.einsum('de,ikd->eik', w_ab, x_ln, preferred_element_type=jnp.float32)  162 us
    convert_element_type x6, local copies, waits for them, and re-layouts, tri_update(): jnp.einsum(einsum_form, ab_cols[0], ab_cols[1], preferred_element_type=jn...  105 us
    dot_general x6, matrix products, finish_update(): jnp.einsum('cij,cd->ijd', y_ln, w_out, preferred_element_type=jnp.float32)  103 us
    convert_element_type x11, local copies, waits for them, and re-layouts, finish_update(): layer_norm(tri_rows.astype(jnp.float32), gain_vec, shift_vec, 0)  102 us
  transfers between devices with their start and end apart: 6, of which 6 were waited for; matrix products, arithmetic and copies ran while one was open for 2% of the time, Pallas kernels for 0%

commit v1 on v0

v1 whole, which is shorter than its diff:
```python
import functools

import jax
import jax.numpy as jnp
from jax import lax
from jax.experimental import pallas as pl
from jax.experimental.pallas import tpu as pltpu
from jax.sharding import PartitionSpec as P

LN_EPS = 1e-5
ROW_AXES = ("dap2", "dap")
ALL_ROWS = ("data", "dap2", "dap")
CHUNKS = 2
ROWS = 16
LANES = 128
F32, BF16 = jnp.float32, jnp.bfloat16


def channel_norm(values, gain, shift):
    mean_val = jnp.mean(values, axis=0, keepdims=True)
    centered = values - mean_val
    var_val = jnp.mean(centered * centered, axis=0, keepdims=True)
    return centered * lax.rsqrt(var_val + LN_EPS) * gain + shift


def sigmoid(values):
    return 1.0 / (1.0 + jnp.exp(-values))


def local_kernel(*refs, first, last, parts):
    refs = list(refs)
    z_ref = refs.pop(0)
    if not first:
        t_ref, gain_in, shift_in, gain_out, shift_out, wg_ref, wo_ref = refs[:7]
        refs = refs[7:]
    if not last:
        mask_ref, gain_nx, shift_nx, wab_ref = refs[:4]
        refs = refs[4:]
    if last and parts > 1:
        refs.pop(0)
    z_out = refs.pop(0)
    ab_out = None if last else refs.pop(0)
    t_scr = None if first else refs.pop(0)
    ab_scr = None if last else refs.pop(0)
    rows = z_ref.shape[0]
    cols = z_out.shape[1] if last else z_out.shape[2]
    blocks = cols // LANES
    hid = wab_ref.shape[0] // 4 if not last else wo_ref.shape[1]

    if not first:
        stride_t = t_scr.shape[1] // hid
        for blk in range(blocks):
            lanes = pl.ds(blk * LANES, LANES)

            def add_up(c, total):
                return total + t_ref[c, :, lanes].astype(F32)

            mean_val = lax.fori_loop(0, hid, add_up, jnp.zeros((rows, LANES), F32), unroll=8) * (1.0 / hid)

            def add_sq(c, total):
                centered = t_ref[c, :, lanes].astype(F32) - mean_val
                return total + centered * centered

            var_val = lax.fori_loop(0, hid, add_sq, jnp.zeros((rows, LANES), F32), unroll=8) * (1.0 / hid)
            scale = lax.rsqrt(var_val + LN_EPS)

            def put(c, carry):
                start = pl.multiple_of(c * stride_t, 8)
                t_scr[blk, pl.ds(start, rows), :] = (t_ref[c, :, lanes].astype(F32) - mean_val) * scale
                return carry

            lax.fori_loop(0, hid, put, 0, unroll=8)

    def one_row(r, carry):
        if first:
            z_val = z_ref[r].astype(F32).T.astype(BF16)
        else:
            z_val = z_ref[r]
        z_f = z_val.astype(F32)
        if not first:
            x_ln = channel_norm(z_f, gain_in[...], shift_in[...]).astype(BF16)
            t_n = [t_scr[blk, pl.ds(r, hid, stride=stride_t), :] for blk in range(blocks)]
            t_n = jnp.concatenate(t_n, axis=1) if blocks > 1 else t_n[0]
            y_ln = (t_n * gain_out[...] + shift_out[...]).astype(BF16)
            update_val = jnp.dot(wo_ref[...], y_ln, preferred_element_type=F32)
            gate_val = sigmoid(jnp.dot(wg_ref[...], x_ln, preferred_element_type=F32))
            z_f = z_f + gate_val * update_val
            if last:
                z_out[r] = z_f.T.astype(BF16)
                return carry
            z_val = z_f.astype(BF16)
            z_f = z_val.astype(F32)
        z_out[r] = z_val
        x_nx = channel_norm(z_f, gain_nx[...], shift_nx[...]).astype(BF16)
        m_row = mask_ref[pl.ds(r, 1), :].astype(F32)
        stride_ab = ab_scr.shape[1] // rows
        for half in range(2):
            proj = jnp.dot(wab_ref[pl.ds(half * 2 * hid, 2 * hid), :], x_nx, preferred_element_type=F32)
            val = m_row * sigmoid(proj[hid:]) * proj[:hid]
            start = pl.multiple_of(r * stride_ab + half * hid, 8)
            for blk in range(blocks):
                ab_scr[blk, pl.ds(start, hid), :] = val[:, blk * LANES : (blk + 1) * LANES]
        return carry

    lax.fori_loop(0, rows, one_row, 0)

    if not last:
        dests, per_dest = ab_out.shape[0], ab_out.shape[1] // 2
        stride_ab = ab_scr.shape[1] // rows

        def send_rows(d, carry):
            for half in range(2):
                for e in range(per_dest):
                    for blk in range(blocks):
                        val = ab_scr[blk, pl.ds(half * hid + d * per_dest + e, rows, stride=stride_ab), :]
                        ab_out[d, half * per_dest + e, :, pl.ds(blk * LANES, LANES)] = val.astype(BF16)
            return carry

        lax.fori_loop(0, dests, send_rows, 0)


def local_call(z_in, t_in, mask_loc, prev, nxt, chunk, out_full, n_dev, width):
    first, last = prev is None, nxt is None
    rows_loc = mask_loc.shape[0]
    chan = z_in.shape[2] if first else z_in.shape[1]
    hid = chan if first else t_in.shape[0]
    wb = min(2 * LANES, width)
    nw = width // wb
    grid = (rows_loc // ROWS, nw)
    whole = lambda arr: pl.BlockSpec(arr.shape, lambda i, j: (0,) * arr.ndim)
    args, specs = [z_in], []
    if first:
        specs.append(pl.BlockSpec((ROWS, wb, chan), lambda i, j: (i, chunk * nw + j, 0)))
    else:
        specs.append(pl.BlockSpec((ROWS, chan, wb), lambda i, j: (i, 0, j)))
        args.append(t_in)
        specs.append(pl.BlockSpec((hid, ROWS, wb), lambda i, j: (0, i, j)))
        args += list(prev)
        specs += [whole(arr) for arr in prev]
    if not last:
        args.append(mask_loc)
        specs.append(pl.BlockSpec((ROWS, wb), lambda i, j: (i, chunk * nw + j)))
        args += list(nxt)
        specs += [whole(arr) for arr in nxt]
    alias = {}
    if last:
        parts = 1 if out_full is None else 2
        if out_full is not None:
            alias = {len(args): 0}
            args.append(out_full)
            specs.append(pl.BlockSpec(memory_space=pl.ANY))
        out_shape = jax.ShapeDtypeStruct((rows_loc, mask_loc.shape[1], chan), BF16)
        out_specs = pl.BlockSpec((ROWS, wb, chan), lambda i, j: (i, chunk * nw + j, 0))
    else:
        parts = 1
        per = 2 * hid // n_dev
        out_shape = (
            jax.ShapeDtypeStruct((rows_loc, chan, width), BF16),
            jax.ShapeDtypeStruct((n_dev, per, rows_loc, width), BF16),
        )
        out_specs = (
            pl.BlockSpec((ROWS, chan, wb), lambda i, j: (i, 0, j)),
            pl.BlockSpec((n_dev, per, ROWS, wb), lambda i, j: (0, 0, i, j)),
        )
    scratch = []
    if not first:
        scratch.append(pltpu.VMEM((wb // LANES, hid * (ROWS + 8), LANES), F32))
    if not last:
        scratch.append(pltpu.VMEM((wb // LANES, ROWS * (2 * hid + 8), LANES), F32))
    pos = rows_loc * width
    flops = 2 * pos * chan * ((0 if first else 2 * hid) + (0 if last else 4 * hid))
    return pl.pallas_call(
        functools.partial(local_kernel, first=first, last=last, parts=parts),
        grid=grid,
        in_specs=specs,
        out_specs=out_specs,
        out_shape=out_shape,
        scratch_shapes=scratch,
        input_output_aliases=alias,
        compiler_params=pltpu.CompilerParams(vmem_limit_bytes=60 * 2**20),
        cost_estimate=pl.CostEstimate(flops=flops, bytes_accessed=6 * pos * chan, transcendentals=0),
        name=f"local_{chunk}",
    )(*args)


def out_kernel(*refs, chunks):
    t_ref = refs[-1]
    total = None
    for p in range(chunks):
        a_val = refs[p][...].reshape(-1, refs[p].shape[-1])
        b_val = refs[chunks + p][...].reshape(-1, refs[chunks + p].shape[-1])
        part = lax.dot_general(a_val, b_val, (((1,), (1,)), ((), ())), preferred_element_type=F32)
        total = part if total is None else total + part
    t_ref[...] = total.astype(BF16).reshape(t_ref.shape)


def in_kernel(*refs, chunks):
    b_ref, t_ref = refs[chunks], refs[-1]
    b_val = b_ref[...].reshape(-1, b_ref.shape[-1])
    n_dev, _, rows, _ = t_ref.shape
    share = n_dev // chunks
    for p in range(chunks):
        a_val = refs[p][...].reshape(-1, refs[p].shape[-1])
        part = lax.dot_general(a_val, b_val, (((0,), (0,)), ((), ())), preferred_element_type=F32)
        t_ref[p * share : (p + 1) * share] = part.astype(BF16).reshape(share, 1, rows, t_ref.shape[-1])


def tri_call(ab_cols, q, outgoing):
    chunks = len(ab_cols)
    n_dev, per, rows, width = ab_cols[0].shape
    per //= 2
    a_spec = pl.BlockSpec((n_dev, 1, rows, width), lambda c: (0, c, 0, 0))
    if outgoing:
        body = out_kernel
        args = list(ab_cols) + list(ab_cols)
        b_spec = pl.BlockSpec((n_dev // chunks, 1, rows, width), lambda c: (q, per + c, 0, 0))
        specs = [a_spec] * chunks + [b_spec] * chunks
    else:
        body = in_kernel
        args = list(ab_cols) + [ab_cols[q]]
        specs = [a_spec] * chunks + [pl.BlockSpec((n_dev, 1, rows, width), lambda c: (0, per + c, 0, 0))]
    size = n_dev * rows
    return pl.pallas_call(
        functools.partial(body, chunks=chunks),
        grid=(per,),
        in_specs=specs,
        out_specs=pl.BlockSpec((n_dev, 1, rows, width), lambda c: (0, c, 0, 0)),
        out_shape=jax.ShapeDtypeStruct((n_dev, per, rows, width), BF16),
        compiler_params=pltpu.CompilerParams(vmem_limit_bytes=60 * 2**20),
        cost_estimate=pl.CostEstimate(
            flops=2 * per * size * size * width, bytes_accessed=6 * per * size * width, transcendentals=0
        ),
        name=f"tri_{q}",
    )(*args)


def exchange(blocks):
    flat = blocks.reshape(blocks.shape[0], -1, blocks.shape[-1])
    return lax.all_to_all(flat, ROW_AXES, 0, 0, tiled=True).reshape(blocks.shape)


def solution(mesh):
    n_dev = mesh.shape["dap2"] * mesh.shape["dap"]
    row_spec = P(ALL_ROWS, None, None)
    mask_spec = P(ALL_ROWS, None)

    def local_stack(pair_rep, pair_mask, norm_in, norm_out, w_ab, w_gate, w_out):
        width = pair_rep.shape[1] // CHUNKS
        wb = min(2 * LANES, width)

        def spread(vec):
            return jnp.broadcast_to(vec.astype(F32)[:, None], (vec.shape[0], wb))

        steps = [(layer, upd) for layer in range(w_ab.shape[0]) for upd in range(2)]

        def before(s):
            l, u = steps[s]
            return (spread(norm_in[l, u, 0]), spread(norm_in[l, u, 1]), w_ab[l, u].T)

        def after(s):
            l, u = steps[s]
            gains = tuple(spread(v) for v in (norm_in[l, u, 0], norm_in[l, u, 1], norm_out[l, u, 0], norm_out[l, u, 1]))
            return gains + (w_gate[l, u].T, w_out[l, u].T)

        z_cur, ab_cols = [None] * CHUNKS, [None] * CHUNKS
        for p in range(CHUNKS):
            z_cur[p], ab = local_call(pair_rep, None, pair_mask, None, before(0), p, None, n_dev, width)
            ab_cols[p] = exchange(ab)
        out = None
        for s, (_, upd) in enumerate(steps):
            t_rows = []
            for q in range(CHUNKS):
                t_recv = exchange(tri_call(ab_cols, q, upd == 0))
                t_rows.append(t_recv.reshape(-1, *t_recv.shape[2:]))
            nxt = before(s + 1) if s + 1 < len(steps) else None
            new_ab = []
            for p in range(CHUNKS):
                res = local_call(z_cur[p], t_rows[p], pair_mask, after(s), nxt, p, out, n_dev, width)
                if nxt is None:
                    out = res
                else:
                    z_cur[p] = res[0]
                    new_ab.append(exchange(res[1]))
            ab_cols = new_ab
        return out

    return jax.shard_map(local_stack, mesh=mesh, in_specs=(row_spec, mask_spec, P(), P(), P(), P(), P()), out_specs=row_spec, check_vma=False)
```

time: 3490 us -> 2200 us (0.63)
  Pallas kernels: 0 us -> 724 us
  blocking collectives: 1220 us -> 623 us
  local copies, waits for them, and re-layouts: 607 us -> 33.8 us
  other arithmetic: 551 us -> 1.98 us
  matrix products: 431 us -> 0 us
  waiting for transfers between devices: 598 us -> 726 us
    pallas_call x0 -> x26, Pallas kernels: none -> 724 us  [the longest x14 613 us: local_call(): pl.pallas_call(functools.partial(local_kernel, first=first, last=last, pa...]
    all_to_all x6, blocking collectives: 1220 us -> 623 us  [exchange(): lax.all_to_all(flat, ROW_AXES, 0, 0, tiled=True).reshape(blocks.shape)]
    dot_general x24 -> x0, matrix products: 431 us -> none  [the longest x6 162 us: row_inputs(): jnp.einsum('de,ikd->eik', w_ab, x_ln, preferred_element_type=jnp.float32)]
    convert_element_type x15 -> x2, other arithmetic: 415 us -> 1.98 us  [spread(): return jnp.broadcast_to(vec.astype(F32)[:, None], (vec.shape[0], wb))]
    slice x18 -> x3, local copies, waits for them, and re-layouts: 351 us -> 3.21 us  [the longest x1 1.95 us: before(): return (spread(norm_in[l, u, 0]), spread(norm_in[l, u, 1]), w_ab[l, u].T)]
    convert_element_type x32 -> x0, local copies, waits for them, and re-layouts: 220 us -> none  [the longest x6 105 us: tri_update(): jnp.einsum(einsum_form, ab_cols[0], ab_cols[1], preferred_element_type=jn...]
    reduce_sum x19 -> x0, other arithmetic: 135 us -> none  [the longest x12 88.5 us: layer_norm(): var_val = jnp.mean(centered * centered, axis=norm_axis, keepdims=True)]
    all_to_all x6 -> x18, waiting for transfers between devices: 598 us -> 726 us  [exchange(): lax.all_to_all(flat, ROW_AXES, 0, 0, tiled=True).reshape(blocks.shape)]
  transfers between devices with their start and end apart: 6 -> 18, of which waited for: 6 -> 18; matrix products, arithmetic and copies ran while one was open for 2% -> 1% of each run, Pallas kernels for 0% -> 28%
where the time goes in v1:
time: 2200 us
  waiting for transfers between devices  726 us (33%)
  Pallas kernels  724 us (33%)
  blocking collectives  623 us (28%)
  starting transfers between devices  89.2 us (4%)
  local copies, waits for them, and re-layouts  33.8 us (2%)
    all_to_all x18, waiting for transfers between devices, exchange(): lax.all_to_all(flat, ROW_AXES, 0, 0, tiled=True).reshape(blocks.shape)  726 us
    all_to_all x6, blocking collectives, exchange(): lax.all_to_all(flat, ROW_AXES, 0, 0, tiled=True).reshape(blocks.shape)  623 us
    pallas_call x14, Pallas kernels, local_call(): pl.pallas_call(functools.partial(local_kernel, first=first, last=last, pa...  613 us
    pallas_call x12, Pallas kernels, tri_call(): pl.pallas_call(functools.partial(body, chunks=chunks), grid=(per,), in_sp...  110 us
    all_to_all x18, starting transfers between devices, exchange(): lax.all_to_all(flat, ROW_AXES, 0, 0, tiled=True).reshape(blocks.shape)  89.2 us
  transfers between devices with their start and end apart: 18, of which 18 were waited for; matrix products, arithmetic and copies ran while one was open for 1% of the time, Pallas kernels for 28%

profile of v1, /device:TPU:103, one launch (start us, length us, event | category | flops | bytes accessed | tf_op | source)
XLA Modules:
  0.0 2198.5 jit_solution(8788494137323908103)
XLA Ops:
  5.6 33.3 %local_0.7 = (bf16[32,128,512]{2,1,0:T(8,128)(2,1)}, bf16[32,8,32,512]{3,2,1,0:T(8,128)(2,1)}) custom-call(bf16[32,1024,128]{2,1,0:T(8,128)(2,1)} %refs_0_.3, s32[32,1024]{1,0:T(8,128)} %refs_8_.19, f32[128,256]{1,0:T(8,128)} %broadcast_in_dim.48.refs_2_, f32[128,256]{1,0:T(8,128)} %broadcast_in_dim.49.refs_3_, bf16[512,128]{1,0:T(8,128)(2,1)} %bitcast.219), custom_call_target="tpu_custom_call" | custom-call | flops 2147483648 | bytes 12582912 | tf_op jit(solution)/shard_map/local_0/pallas_call | solution.py:172
  38.9 8.0 all-to-all-start
  46.9 33.3 %local_1.7 = (bf16[32,128,512]{2,1,0:T(8,128)(2,1)}, bf16[32,8,32,512]{3,2,1,0:T(8,128)(2,1)}) custom-call(bf16[32,1024,128]{2,1,0:T(8,128)(2,1)} %refs_0_.3, s32[32,1024]{1,0:T(8,128)} %refs_8_.19, f32[128,256]{1,0:T(8,128)} %broadcast_in_dim.48.refs_2_, f32[128,256]{1,0:T(8,128)} %broadcast_in_dim.49.refs_3_, bf16[512,128]{1,0:T(8,128)(2,1)} %bitcast.220), custom_call_target="tpu_custom_call" | custom-call | flops 2147483648 | bytes 12582912 | tf_op jit(solution)/shard_map/local_1/pallas_call | solution.py:172
  80.2 79.8 %all-to-all-done = bf16[32,256,512]{2,1,0:T(8,128)(2,1)} async-done(((bf16[32,256,512]{2,1,0:T(8,128)(2,1)}), bf16[32,256,512]{2,1,0:T(8,128)(2,1)}, u32[]{:S(2)}, u32[]{:S(2)}) %all-to-all-start) | async-done | bytes 8388640 | tf_op jit(solution)/shard_map/all_to_all | solution.py:239
  160.0 103.9 %all_to_all.120 = bf16[32,256,512]{2,1,0:T(8,128)(2,1)} all-to-all(bf16[32,256,512]{2,1,0:T(8,128)(2,1)} %bitcast.218), channel_id=1, replica_groups=mesh['data'=1,'dap2'=4,'dap'=8] {'dap2','dap'}, dimensions={0} | all-to-all | bytes 16777216 | tf_op jit(solution)/shard_map/all_to_all | solution.py:239
  263.9 9.2 tri_1.6
  273.1 6.3 all-to-all-start.2
  279.4 9.2 tri_0.6
  288.5 48.2 %all-to-all-done.2 = bf16[32,128,512]{2,1,0:T(8,128)(2,1)} async-done(((bf16[32,128,512]{2,1,0:T(8,128)(2,1)}), bf16[32,128,512]{2,1,0:T(8,128)(2,1)}, u32[]{:S(2)}, u32[]{:S(2)}) %all-to-all-start.2) | async-done | bytes 4194336 | tf_op jit(solution)/shard_map/all_to_all | solution.py:239
  336.8 3.9 all-to-all-start.3
  347.6 48.9 %local_1.8 = (bf16[32,128,512]{2,1,0:T(8,128)(2,1)}, bf16[32,8,32,512]{3,2,1,0:T(8,128)(2,1)}) custom-call(bf16[32,128,512]{2,1,0:T(8,128)(2,1)} %get-tuple-element.29.refs_0_, bf16[128,32,512]{2,1,0:T(8,128)(2,1)} %bitcast.10.refs_1_, f32[128,256]{1,0:T(8,128)} %broadcast_in_dim.48.refs_2_, f32[128,256]{1,0:T(8,128)} %broadcast_in_dim.49.refs_3_, ...), custom_call_target="tpu_custom_call" | custom-call | flops 3221225472 | bytes 12582912 | tf_op jit(solution)/shard_map/local_1/pallas_call | solution.py:172
  397.5 5.2 all-to-all-start.5
  402.7 49.0 %local_0.8 = (bf16[32,128,512]{2,1,0:T(8,128)(2,1)}, bf16[32,8,32,512]{3,2,1,0:T(8,128)(2,1)}) custom-call(bf16[32,128,512]{2,1,0:T(8,128)(2,1)} %get-tuple-element.33.refs_0_, bf16[128,32,512]{2,1,0:T(8,128)(2,1)} %bitcast.22.refs_1_, f32[128,256]{1,0:T(8,128)} %broadcast_in_dim.48.refs_2_, f32[128,256]{1,0:T(8,128)} %broadcast_in_dim.49.refs_3_, ...), custom_call_target="tpu_custom_call" | custom-call | flops 3221225472 | bytes 12582912 | tf_op jit(solution)/shard_map/local_0/pallas_call | solution.py:172
  451.7 64.1 %all-to-all-done.5 = bf16[32,256,512]{2,1,0:T(8,128)(2,1)} async-done(((bf16[32,256,512]{2,1,0:T(8,128)(2,1)}), bf16[32,256,512]{2,1,0:T(8,128)(2,1)}, u32[]{:S(2)}, u32[]{:S(2)}) %all-to-all-start.5) | async-done | bytes 8388640 | tf_op jit(solution)/shard_map/all_to_all | solution.py:239
  515.9 103.9 %all_to_all.121 = bf16[32,256,512]{2,1,0:T(8,128)(2,1)} all-to-all(bf16[32,256,512]{2,1,0:T(8,128)(2,1)} %bitcast.212), channel_id=1, replica_groups=mesh['data'=1,'dap2'=4,'dap'=8] {'dap2','dap'}, dimensions={0} | all-to-all | bytes 16777216 | tf_op jit(solution)/shard_map/all_to_all | solution.py:239
  619.8 9.2 tri_1.7
  629.0 6.3 all-to-all-start.6
  635.2 9.2 tri_0.7
  644.5 48.2 %all-to-all-done.6 = bf16[32,128,512]{2,1,0:T(8,128)(2,1)} async-done(((bf16[32,128,512]{2,1,0:T(8,128)(2,1)}), bf16[32,128,512]{2,1,0:T(8,128)(2,1)}, u32[]{:S(2)}, u32[]{:S(2)}) %all-to-all-start.6) | async-done | bytes 4194336 | tf_op jit(solution)/shard_map/all_to_all | solution.py:239
  692.6 3.7 all-to-all-start.7
  701.5 48.9 %local_1.9 = (bf16[32,128,512]{2,1,0:T(8,128)(2,1)}, bf16[32,8,32,512]{3,2,1,0:T(8,128)(2,1)}) custom-call(bf16[32,128,512]{2,1,0:T(8,128)(2,1)} %get-tuple-element.32.refs_0_, bf16[128,32,512]{2,1,0:T(8,128)(2,1)} %bitcast.31.refs_1_, f32[128,256]{1,0:T(8,128)} %broadcast_in_dim.52.refs_9_.refs_2_, f32[128,256]{1,0:T(8,128)} %broadcast_in_dim.53.refs_10_.refs_3_, ...), custom_call_target="tpu_custom_call" | custom-call | flops 3221225472 | bytes 12582912 | tf_op jit(solution)/shard_map/local_1/pallas_call | solution.py:172
  753.3 3.9 all-to-all-start.9
  757.2 49.0 %local_0.9 = (bf16[32,128,512]{2,1,0:T(8,128)(2,1)}, bf16[32,8,32,512]{3,2,1,0:T(8,128)(2,1)}) custom-call(bf16[32,128,512]{2,1,0:T(8,128)(2,1)} %get-tuple-element.37.refs_0_, bf16[128,32,512]{2,1,0:T(8,128)(2,1)} %bitcast.43.refs_1_, f32[128,256]{1,0:T(8,128)} %broadcast_in_dim.52.refs_9_.refs_2_, f32[128,256]{1,0:T(8,128)} %broadcast_in_dim.53.refs_10_.refs_3_, ...), custom_call_target="tpu_custom_call" | custom-call | flops 3221225472 | bytes 12582912 | tf_op jit(solution)/shard_map/local_0/pallas_call | solution.py:172
  806.2 63.8 %all-to-all-done.9 = bf16[32,256,512]{2,1,0:T(8,128)(2,1)} async-done(((bf16[32,256,512]{2,1,0:T(8,128)(2,1)}), bf16[32,256,512]{2,1,0:T(8,128)(2,1)}, u32[]{:S(2)}, u32[]{:S(2)}) %all-to-all-start.9) | async-done | bytes 8388640 | tf_op jit(solution)/shard_map/all_to_all | solution.py:239
  870.0 103.9 %all_to_all.122 = bf16[32,256,512]{2,1,0:T(8,128)(2,1)} all-to-all(bf16[32,256,512]{2,1,0:T(8,128)(2,1)} %bitcast.213), channel_id=1, replica_groups=mesh['data'=1,'dap2'=4,'dap'=8] {'dap2','dap'}, dimensions={0} | all-to-all | bytes 16777216 | tf_op jit(solution)/shard_map/all_to_all | solution.py:239
  973.9 9.1 tri_1.8
  983.0 6.3 all-to-all-start.10
  989.3 9.2 tri_0.8
  998.5 48.2 %all-to-all-done.10 = bf16[32,128,512]{2,1,0:T(8,128)(2,1)} async-done(((bf16[32,128,512]{2,1,0:T(8,128)(2,1)}), bf16[32,128,512]{2,1,0:T(8,128)(2,1)}, u32[]{:S(2)}, u32[]{:S(2)}) %all-to-all-start.10) | async-done | bytes 4194336 | tf_op jit(solution)/shard_map/all_to_all | solution.py:239
  1046.7 3.7 all-to-all-start.11
  1055.5 48.9 %local_1.10 = (bf16[32,128,512]{2,1,0:T(8,128)(2,1)}, bf16[32,8,32,512]{3,2,1,0:T(8,128)(2,1)}) custom-call(bf16[32,128,512]{2,1,0:T(8,128)(2,1)} %get-tuple-element.36.refs_0_, bf16[128,32,512]{2,1,0:T(8,128)(2,1)} %bitcast.52.refs_1_, f32[128,256]{1,0:T(8,128)} %broadcast_in_dim.56.refs_9_.refs_2_, f32[128,256]{1,0:T(8,128)} %broadcast_in_dim.57.refs_10_.refs_3_, ...), custom_call_target="tpu_custom_call" | custom-call | flops 3221225472 | bytes 12582912 | tf_op jit(solution)/shard_map/local_1/pallas_call | solution.py:172
  1104.4 2.9 all-to-all-done.11
  1107.3 3.9 all-to-all-start.13
  1111.2 49.0 %local_0.10 = (bf16[32,128,512]{2,1,0:T(8,128)(2,1)}, bf16[32,8,32,512]{3,2,1,0:T(8,128)(2,1)}) custom-call(bf16[32,128,512]{2,1,0:T(8,128)(2,1)} %get-tuple-element.41.refs_0_, bf16[128,32,512]{2,1,0:T(8,128)(2,1)} %bitcast.64.refs_1_, f32[128,256]{1,0:T(8,128)} %broadcast_in_dim.56.refs_9_.refs_2_, f32[128,256]{1,0:T(8,128)} %broadcast_in_dim.57.refs_10_.refs_3_, ...), custom_call_target="tpu_custom_call" | custom-call | flops 3221225472 | bytes 12582912 | tf_op jit(solution)/shard_map/local_0/pallas_call | solution.py:172
  1160.2 63.8 %all-to-all-done.13 = bf16[32,256,512]{2,1,0:T(8,128)(2,1)} async-done(((bf16[32,256,512]{2,1,0:T(8,128)(2,1)}), bf16[32,256,512]{2,1,0:T(8,128)(2,1)}, u32[]{:S(2)}, u32[]{:S(2)}) %all-to-all-start.13) | async-done | bytes 8388640 | tf_op jit(solution)/shard_map/all_to_all | solution.py:239
  1224.0 103.9 %all_to_all.123 = bf16[32,256,512]{2,1,0:T(8,128)(2,1)} all-to-all(bf16[32,256,512]{2,1,0:T(8,128)(2,1)} %bitcast.214), channel_id=1, replica_groups=mesh['data'=1,'dap2'=4,'dap'=8] {'dap2','dap'}, dimensions={0} | all-to-all | bytes 16777216 | tf_op jit(solution)/shard_map/all_to_all | solution.py:239
  1327.9 9.2 tri_1.9
  1337.1 6.3 all-to-all-start.14
  1343.4 9.2 tri_0.9
  1352.6 48.2 %all-to-all-done.14 = bf16[32,128,512]{2,1,0:T(8,128)(2,1)} async-done(((bf16[32,128,512]{2,1,0:T(8,128)(2,1)}), bf16[32,128,512]{2,1,0:T(8,128)(2,1)}, u32[]{:S(2)}, u32[]{:S(2)}) %all-to-all-start.14) | async-done | bytes 4194336 | tf_op jit(solution)/shard_map/all_to_all | solution.py:239
  1400.8 3.9 all-to-all-start.15
  1409.8 48.9 %local_1.11 = (bf16[32,128,512]{2,1,0:T(8,128)(2,1)}, bf16[32,8,32,512]{3,2,1,0:T(8,128)(2,1)}) custom-call(bf16[32,128,512]{2,1,0:T(8,128)(2,1)} %get-tuple-element.40.refs_0_, bf16[128,32,512]{2,1,0:T(8,128)(2,1)} %bitcast.73.refs_1_, f32[128,256]{1,0:T(8,128)} %broadcast_in_dim.60.refs_9_.refs_2_, f32[128,256]{1,0:T(8,128)} %broadcast_in_dim.61.refs_10_.refs_3_, ...), custom_call_target="tpu_custom_call" | custom-call | flops 3221225472 | bytes 12582912 | tf_op jit(solution)/shard_map/local_1/pallas_call | solution.py:172
  1461.6 3.9 all-to-all-start.17
  1465.5 49.0 %local_0.11 = (bf16[32,128,512]{2,1,0:T(8,128)(2,1)}, bf16[32,8,32,512]{3,2,1,0:T(8,128)(2,1)}) custom-call(bf16[32,128,512]{2,1,0:T(8,128)(2,1)} %get-tuple-element.45.refs_0_, bf16[128,32,512]{2,1,0:T(8,128)(2,1)} %bitcast.85.refs_1_, f32[128,256]{1,0:T(8,128)} %broadcast_in_dim.60.refs_9_.refs_2_, f32[128,256]{1,0:T(8,128)} %broadcast_in_dim.61.refs_10_.refs_3_, ...), custom_call_target="tpu_custom_call" | custom-call | flops 3221225472 | bytes 12582912 | tf_op jit(solution)/shard_map/local_0/pallas_call | solution.py:172
  1514.5 63.8 %all-to-all-done.17 = bf16[32,256,512]{2,1,0:T(8,128)(2,1)} async-done(((bf16[32,256,512]{2,1,0:T(8,128)(2,1)}), bf16[32,256,512]{2,1,0:T(8,128)(2,1)}, u32[]{:S(2)}, u32[]{:S(2)}) %all-to-all-start.17) | async-done | bytes 8388640 | tf_op jit(solution)/shard_map/all_to_all | solution.py:239
  1578.3 103.9 %all_to_all.124 = bf16[32,256,512]{2,1,0:T(8,128)(2,1)} all-to-all(bf16[32,256,512]{2,1,0:T(8,128)(2,1)} %bitcast.215), channel_id=1, replica_groups=mesh['data'=1,'dap2'=4,'dap'=8] {'dap2','dap'}, dimensions={0} | all-to-all | bytes 16777216 | tf_op jit(solution)/shard_map/all_to_all | solution.py:239
  1682.2 9.1 tri_1.10
  1691.3 6.3 all-to-all-start.18
  1697.6 9.2 tri_0.10
  1706.8 48.2 %all-to-all-done.18 = bf16[32,128,512]{2,1,0:T(8,128)(2,1)} async-done(((bf16[32,128,512]{2,1,0:T(8,128)(2,1)}), bf16[32,128,512]{2,1,0:T(8,128)(2,1)}, u32[]{:S(2)}, u32[]{:S(2)}) %all-to-all-start.18) | async-done | bytes 4194336 | tf_op jit(solution)/shard_map/all_to_all | solution.py:239
  1755.0 3.9 all-to-all-start.19
  1764.1 48.9 %local_1.12 = (bf16[32,128,512]{2,1,0:T(8,128)(2,1)}, bf16[32,8,32,512]{3,2,1,0:T(8,128)(2,1)}) custom-call(bf16[32,128,512]{2,1,0:T(8,128)(2,1)} %get-tuple-element.44.refs_0_, bf16[128,32,512]{2,1,0:T(8,128)(2,1)} %bitcast.94.refs_1_, f32[128,256]{1,0:T(8,128)} %broadcast_in_dim.64.refs_9_.refs_2_, f32[128,256]{1,0:T(8,128)} %broadcast_in_dim.65.refs_10_.refs_3_, ...), custom_call_target="tpu_custom_call" | custom-call | flops 3221225472 | bytes 12582912 | tf_op jit(solution)/shard_map/local_1/pallas_call | solution.py:172
  1815.9 3.9 all-to-all-start.21
  1819.7 49.1 %local_0.12 = (bf16[32,128,512]{2,1,0:T(8,128)(2,1)}, bf16[32,8,32,512]{3,2,1,0:T(8,128)(2,1)}) custom-call(bf16[32,128,512]{2,1,0:T(8,128)(2,1)} %get-tuple-element.49.refs_0_, bf16[128,32,512]{2,1,0:T(8,128)(2,1)} %bitcast.106.refs_1_, f32[128,256]{1,0:T(8,128)} %broadcast_in_dim.64.refs_9_.refs_2_, f32[128,256]{1,0:T(8,128)} %broadcast_in_dim.65.refs_10_.refs_3_, ...), custom_call_target="tpu_custom_call" | custom-call | flops 3221225472 | bytes 12582912 | tf_op jit(solution)/shard_map/local_0/pallas_call | solution.py:172
  1868.8 63.8 %all-to-all-done.21 = bf16[32,256,512]{2,1,0:T(8,128)(2,1)} async-done(((bf16[32,256,512]{2,1,0:T(8,128)(2,1)}), bf16[32,256,512]{2,1,0:T(8,128)(2,1)}, u32[]{:S(2)}, u32[]{:S(2)}) %all-to-all-start.21) | async-done | bytes 8388640 | tf_op jit(solution)/shard_map/all_to_all | solution.py:239
  1932.5 103.9 %all_to_all.125 = bf16[32,256,512]{2,1,0:T(8,128)(2,1)} all-to-all(bf16[32,256,512]{2,1,0:T(8,128)(2,1)} %bitcast.216), channel_id=1, replica_groups=mesh['data'=1,'dap2'=4,'dap'=8] {'dap2','dap'}, dimensions={0} | all-to-all | bytes 16777216 | tf_op jit(solution)/shard_map/all_to_all | solution.py:239
  2036.4 9.2 tri_0.11
  2045.7 6.3 all-to-all-start.23
  2051.9 9.2 tri_1.11
  2061.2 48.2 %all-to-all-done.23 = bf16[32,128,512]{2,1,0:T(8,128)(2,1)} async-done(((bf16[32,128,512]{2,1,0:T(8,128)(2,1)}), bf16[32,128,512]{2,1,0:T(8,128)(2,1)}, u32[]{:S(2)}, u32[]{:S(2)}) %all-to-all-start.23) | async-done | bytes 4194336 | tf_op jit(solution)/shard_map/all_to_all | solution.py:239
  2109.3 3.8 all-to-all-start.22
  2116.1 28.5 %local_0.13.refs_8_ = bf16[32,1024,128]{2,1,0:T(8,128)(2,1)} custom-call(bf16[32,128,512]{2,1,0:T(8,128)(2,1)} %get-tuple-element.52.refs_0_, bf16[128,32,512]{2,1,0:T(8,128)(2,1)} %bitcast.123.refs_1_, f32[128,256]{1,0:T(8,128)} %broadcast_in_dim.68.refs_9_.refs_2_, f32[128,256]{1,0:T(8,128)} %broadcast_in_dim.69.refs_10_.refs_3_, ...), custom_call_target="tpu_custom_call" | custom-call | flops 1073741824 | bytes 12582912 | tf_op jit(solution)/shard_map/local_0/pallas_call | solution.py:172
  2144.5 25.5 %all-to-all-done.22 = bf16[32,128,512]{2,1,0:T(8,128)(2,1)} async-done(((bf16[32,128,512]{2,1,0:T(8,128)(2,1)}), bf16[32,128,512]{2,1,0:T(8,128)(2,1)}, u32[]{:S(2)}, u32[]{:S(2)}) %all-to-all-start.22) | async-done | bytes 4194336 | tf_op jit(solution)/shard_map/all_to_all | solution.py:239
  2170.0 28.5 %local_1.13 = bf16[32,1024,128]{2,1,0:T(8,128)(2,1)} custom-call(bf16[32,128,512]{2,1,0:T(8,128)(2,1)} %get-tuple-element.48.refs_0_, bf16[128,32,512]{2,1,0:T(8,128)(2,1)} %bitcast.115.refs_1_, f32[128,256]{1,0:T(8,128)} %broadcast_in_dim.68.refs_9_.refs_2_, f32[128,256]{1,0:T(8,128)} %broadcast_in_dim.69.refs_10_.refs_3_, ...), custom_call_target="tpu_custom_call", output_to_operand_aliasing={{}: (8, {})} | custom-call | flops 1073741824 | bytes 12582912 | tf_op jit(solution)/shard_map/local_1/pallas_call | solution.py:172
  (85 shorter events, 45.3 us)
Async XLA Ops:
  38.9 121.1 %all-to-all-start = ((bf16[32,256,512]{2,1,0:T(8,128)(2,1)}), bf16[32,256,512]{2,1,0:T(8,128)(2,1)}, u32[]{:S(2)}, u32[]{:S(2)}) async-start(bf16[32,256,512]{2,1,0:T(8,128)(2,1)} %bitcast.217), calls=%async_computation | async-start | bytes 16777216 | tf_op jit(solution)/shard_map/all_to_all | solution.py:239
  273.1 63.7 %all-to-all-start.2 = ((bf16[32,128,512]{2,1,0:T(8,128)(2,1)}), bf16[32,128,512]{2,1,0:T(8,128)(2,1)}, u32[]{:S(2)}, u32[]{:S(2)}) async-start(bf16[32,128,512]{2,1,0:T(8,128)(2,1)} %bitcast.201), calls=%async_computation.2 | async-start | bytes 8388608 | tf_op jit(solution)/shard_map/all_to_all | solution.py:239
  336.8 3.9 copy-start.2
  336.8 5.3 copy-start.3
  336.8 7.3 copy-start.8
  336.8 60.8 %all-to-all-start.3 = ((bf16[32,128,512]{2,1,0:T(8,128)(2,1)}), bf16[32,128,512]{2,1,0:T(8,128)(2,1)}, u32[]{:S(2)}, u32[]{:S(2)}) async-start(bf16[32,128,512]{2,1,0:T(8,128)(2,1)} %bitcast.195), calls=%async_computation.3 | async-start | bytes 8388608 | tf_op jit(solution)/shard_map/all_to_all | solution.py:239
  397.5 118.3 %all-to-all-start.5 = ((bf16[32,256,512]{2,1,0:T(8,128)(2,1)}), bf16[32,256,512]{2,1,0:T(8,128)(2,1)}, u32[]{:S(2)}, u32[]{:S(2)}) async-start(bf16[32,256,512]{2,1,0:T(8,128)(2,1)} %bitcast.207), calls=%async_computation.5 | async-start | bytes 16777216 | tf_op jit(solution)/shard_map/all_to_all | solution.py:239
  629.0 63.7 %all-to-all-start.6 = ((bf16[32,128,512]{2,1,0:T(8,128)(2,1)}), bf16[32,128,512]{2,1,0:T(8,128)(2,1)}, u32[]{:S(2)}, u32[]{:S(2)}) async-start(bf16[32,128,512]{2,1,0:T(8,128)(2,1)} %bitcast.202), calls=%async_computation.6 | async-start | bytes 8388608 | tf_op jit(solution)/shard_map/all_to_all | solution.py:239
  692.6 60.7 %all-to-all-start.7 = ((bf16[32,128,512]{2,1,0:T(8,128)(2,1)}), bf16[32,128,512]{2,1,0:T(8,128)(2,1)}, u32[]{:S(2)}, u32[]{:S(2)}) async-start(bf16[32,128,512]{2,1,0:T(8,128)(2,1)} %bitcast.197), calls=%async_computation.7 | async-start | bytes 8388608 | tf_op jit(solution)/shard_map/all_to_all | solution.py:239
  753.3 116.7 %all-to-all-start.9 = ((bf16[32,256,512]{2,1,0:T(8,128)(2,1)}), bf16[32,256,512]{2,1,0:T(8,128)(2,1)}, u32[]{:S(2)}, u32[]{:S(2)}) async-start(bf16[32,256,512]{2,1,0:T(8,128)(2,1)} %bitcast.208), calls=%async_computation.9 | async-start | bytes 16777216 | tf_op jit(solution)/shard_map/all_to_all | solution.py:239
  983.0 63.7 %all-to-all-start.10 = ((bf16[32,128,512]{2,1,0:T(8,128)(2,1)}), bf16[32,128,512]{2,1,0:T(8,128)(2,1)}, u32[]{:S(2)}, u32[]{:S(2)}) async-start(bf16[32,128,512]{2,1,0:T(8,128)(2,1)} %bitcast.203), calls=%async_computation.10 | async-start | bytes 8388608 | tf_op jit(solution)/shard_map/all_to_all | solution.py:239
  1046.7 60.7 %all-to-all-start.11 = ((bf16[32,128,512]{2,1,0:T(8,128)(2,1)}), bf16[32,128,512]{2,1,0:T(8,128)(2,1)}, u32[]{:S(2)}, u32[]{:S(2)}) async-start(bf16[32,128,512]{2,1,0:T(8,128)(2,1)} %bitcast.198), calls=%async_computation.11 | async-start | bytes 8388608 | tf_op jit(solution)/shard_map/all_to_all | solution.py:239
  1107.3 116.7 %all-to-all-start.13 = ((bf16[32,256,512]{2,1,0:T(8,128)(2,1)}), bf16[32,256,512]{2,1,0:T(8,128)(2,1)}, u32[]{:S(2)}, u32[]{:S(2)}) async-start(bf16[32,256,512]{2,1,0:T(8,128)(2,1)} %bitcast.209), calls=%async_computation.13 | async-start | bytes 16777216 | tf_op jit(solution)/shard_map/all_to_all | solution.py:239
  1337.1 63.7 %all-to-all-start.14 = ((bf16[32,128,512]{2,1,0:T(8,128)(2,1)}), bf16[32,128,512]{2,1,0:T(8,128)(2,1)}, u32[]{:S(2)}, u32[]{:S(2)}) async-start(bf16[32,128,512]{2,1,0:T(8,128)(2,1)} %bitcast.204), calls=%async_computation.14 | async-start | bytes 8388608 | tf_op jit(solution)/shard_map/all_to_all | solution.py:239
  1400.8 5.3 copy-start.1
  1400.8 6.1 copy-start.14
  1400.8 6.8 copy-start.13
  1400.8 60.8 %all-to-all-start.15 = ((bf16[32,128,512]{2,1,0:T(8,128)(2,1)}), bf16[32,128,512]{2,1,0:T(8,128)(2,1)}, u32[]{:S(2)}, u32[]{:S(2)}) async-start(bf16[32,128,512]{2,1,0:T(8,128)(2,1)} %bitcast.199), calls=%async_computation.15 | async-start | bytes 8388608 | tf_op jit(solution)/shard_map/all_to_all | solution.py:239
  1461.6 116.7 %all-to-all-start.17 = ((bf16[32,256,512]{2,1,0:T(8,128)(2,1)}), bf16[32,256,512]{2,1,0:T(8,128)(2,1)}, u32[]{:S(2)}, u32[]{:S(2)}) async-start(bf16[32,256,512]{2,1,0:T(8,128)(2,1)} %bitcast.210), calls=%async_computation.17 | async-start | bytes 16777216 | tf_op jit(solution)/shard_map/all_to_all | solution.py:239
  1691.3 63.7 %all-to-all-start.18 = ((bf16[32,128,512]{2,1,0:T(8,128)(2,1)}), bf16[32,128,512]{2,1,0:T(8,128)(2,1)}, u32[]{:S(2)}, u32[]{:S(2)}) async-start(bf16[32,128,512]{2,1,0:T(8,128)(2,1)} %bitcast.205), calls=%async_computation.18 | async-start | bytes 8388608 | tf_op jit(solution)/shard_map/all_to_all | solution.py:239
  1755.0 4.0 copy-start.6
  1755.0 4.7 copy-start.7
  1755.0 5.4 copy-start
  1755.0 6.2 copy-start.10
  1755.0 6.9 copy-start.9
  1755.0 7.6 copy-start.16
  1755.0 8.3 copy-start.15
  1755.0 60.8 %all-to-all-start.19 = ((bf16[32,128,512]{2,1,0:T(8,128)(2,1)}), bf16[32,128,512]{2,1,0:T(8,128)(2,1)}, u32[]{:S(2)}, u32[]{:S(2)}) async-start(bf16[32,128,512]{2,1,0:T(8,128)(2,1)} %bitcast.196), calls=%async_computation.19 | async-start | bytes 8388608 | tf_op jit(solution)/shard_map/all_to_all | solution.py:239
  1815.9 116.7 %all-to-all-start.21 = ((bf16[32,256,512]{2,1,0:T(8,128)(2,1)}), bf16[32,256,512]{2,1,0:T(8,128)(2,1)}, u32[]{:S(2)}, u32[]{:S(2)}) async-start(bf16[32,256,512]{2,1,0:T(8,128)(2,1)} %bitcast.211), calls=%async_computation.21 | async-start | bytes 16777216 | tf_op jit(solution)/shard_map/all_to_all | solution.py:239
  2045.7 63.7 %all-to-all-start.23 = ((bf16[32,128,512]{2,1,0:T(8,128)(2,1)}), bf16[32,128,512]{2,1,0:T(8,128)(2,1)}, u32[]{:S(2)}, u32[]{:S(2)}) async-start(bf16[32,128,512]{2,1,0:T(8,128)(2,1)} %bitcast.206), calls=%async_computation.23 | async-start | bytes 8388608 | tf_op jit(solution)/shard_map/all_to_all | solution.py:239
  2109.3 3.8 copy-start.4
  2109.3 4.6 copy-start.5
  2109.3 5.3 copy-start.12
  2109.3 6.0 copy-start.11
  2109.3 60.7 %all-to-all-start.22 = ((bf16[32,128,512]{2,1,0:T(8,128)(2,1)}), bf16[32,128,512]{2,1,0:T(8,128)(2,1)}, u32[]{:S(2)}, u32[]{:S(2)}) async-start(bf16[32,128,512]{2,1,0:T(8,128)(2,1)} %bitcast.200), calls=%async_computation.22 | async-start | bytes 8388608 | tf_op jit(solution)/shard_map/all_to_all | solution.py:239

commit v2 on v1

v2 whole, which is shorter than its diff:
```python
import functools

import jax
import jax.numpy as jnp
from jax import lax
from jax.experimental import pallas as pl
from jax.experimental.pallas import tpu as pltpu
from jax.sharding import PartitionSpec as P

LN_EPS = 1e-5
ROW_AXES = ("dap2", "dap")
ALL_ROWS = ("data", "dap2", "dap")
CHUNKS = 2
PIECES = 4
ROWS = 16
LANES = 128
F32, BF16 = jnp.float32, jnp.bfloat16


def channel_norm(values, gain, shift):
    mean_val = jnp.mean(values, axis=0, keepdims=True)
    centered = values - mean_val
    var_val = jnp.mean(centered * centered, axis=0, keepdims=True)
    return centered * lax.rsqrt(var_val + LN_EPS) * gain + shift


def sigmoid(values):
    return 1.0 / (1.0 + jnp.exp(-values))


def finish_and_project(refs, wts, scr, first, last):
    refs = list(refs)
    z_ref = refs.pop(0)
    t_ref = None if first else refs.pop(0)
    mask_ref = None if last else refs.pop(0)
    z_out = refs.pop(0)
    ab_out = None if last else refs.pop(0)
    if not first:
        gain_in, shift_in, gain_out, shift_out, wg_ref, wo_ref = wts[0]
    if not last:
        gain_nx, shift_nx, wab_ref = wts[1]
    t_scr, ab_scr = scr
    rows = z_ref.shape[0]
    cols = z_out.shape[1] if last else z_out.shape[2]
    blocks = cols // LANES
    hid = wab_ref.shape[0] // 4 if not last else wo_ref.shape[1]
    stride_t = t_scr.shape[1] // hid
    stride_ab = ab_scr.shape[1] // rows

    if not first:
        for blk in range(blocks):
            lanes = pl.ds(blk * LANES, LANES)

            def add_up(c, total):
                return total + t_ref[c, :, lanes].astype(F32)

            mean_val = lax.fori_loop(0, hid, add_up, jnp.zeros((rows, LANES), F32), unroll=8) * (1.0 / hid)

            def add_sq(c, total):
                centered = t_ref[c, :, lanes].astype(F32) - mean_val
                return total + centered * centered

            var_val = lax.fori_loop(0, hid, add_sq, jnp.zeros((rows, LANES), F32), unroll=8) * (1.0 / hid)
            scale = lax.rsqrt(var_val + LN_EPS)

            def put(c, carry):
                start = pl.multiple_of(c * stride_t, 8)
                t_scr[blk, pl.ds(start, rows), :] = (t_ref[c, :, lanes].astype(F32) - mean_val) * scale
                return carry

            lax.fori_loop(0, hid, put, 0, unroll=8)

    def one_row(r, carry):
        if first:
            z_val = z_ref[r].astype(F32).T.astype(BF16)
        else:
            z_val = z_ref[r]
        z_f = z_val.astype(F32)
        if not first:
            x_ln = channel_norm(z_f, gain_in[...], shift_in[...]).astype(BF16)
            t_n = [t_scr[blk, pl.ds(r, hid, stride=stride_t), :] for blk in range(blocks)]
            t_n = jnp.concatenate(t_n, axis=1) if blocks > 1 else t_n[0]
            y_ln = (t_n * gain_out[...] + shift_out[...]).astype(BF16)
            update_val = jnp.dot(wo_ref[...], y_ln, preferred_element_type=F32)
            gate_val = sigmoid(jnp.dot(wg_ref[...], x_ln, preferred_element_type=F32))
            z_f = z_f + gate_val * update_val
            if last:
                z_out[r] = z_f.T.astype(BF16)
                return carry
            z_val = z_f.astype(BF16)
            z_f = z_val.astype(F32)
        z_out[r] = z_val
        x_nx = channel_norm(z_f, gain_nx[...], shift_nx[...]).astype(BF16)
        m_row = mask_ref[pl.ds(r, 1), :].astype(F32)
        for half in range(2):
            proj = jnp.dot(wab_ref[pl.ds(half * 2 * hid, 2 * hid), :], x_nx, preferred_element_type=F32)
            val = m_row * sigmoid(proj[hid:]) * proj[:hid]
            start = pl.multiple_of(r * stride_ab + half * hid, 8)
            for blk in range(blocks):
                ab_scr[blk, pl.ds(start, hid), :] = val[:, blk * LANES : (blk + 1) * LANES]
        return carry

    lax.fori_loop(0, rows, one_row, 0)

    if not last:
        dests, per_dest = ab_out.shape[0], ab_out.shape[1] // 2

        def send_rows(d, carry):
            for half in range(2):
                for e in range(per_dest):
                    for blk in range(blocks):
                        val = ab_scr[blk, pl.ds(half * hid + d * per_dest + e, rows, stride=stride_ab), :]
                        ab_out[d, half * per_dest + e, :, pl.ds(blk * LANES, LANES)] = val.astype(BF16)
            return carry

        lax.fori_loop(0, dests, send_rows, 0)


def local_specs(chan, hid, n_dev, wb, nw, chunk, first, last):
    specs = [pl.BlockSpec((ROWS, wb, chan), lambda i, j: (i, chunk * nw + j, 0)) if first else pl.BlockSpec((ROWS, chan, wb), lambda i, j: (i, 0, j))]
    if not first:
        specs.append(pl.BlockSpec((hid, ROWS, wb), lambda i, j: (0, i, j)))
    if last:
        return specs, [pl.BlockSpec((ROWS, wb, chan), lambda i, j: (i, chunk * nw + j, 0))]
    specs.append(pl.BlockSpec((ROWS, wb), lambda i, j: (i, chunk * nw + j)))
    outs = [
        pl.BlockSpec((ROWS, chan, wb), lambda i, j: (i, 0, j)),
        pl.BlockSpec((n_dev, 2 * hid // n_dev, ROWS, wb), lambda i, j: (0, 0, i, j)),
    ]
    return specs, outs


def local_scratch(hid, wb):
    return [
        pltpu.VMEM((wb // LANES, hid * (ROWS + 8), LANES), F32),
        pltpu.VMEM((wb // LANES, ROWS * (2 * hid + 8), LANES), F32),
    ]


def local_call(z_in, t_in, mask_loc, prev, nxt, chunk, out_full, n_dev, width):
    first, last = prev is None, nxt is None
    rows_loc = mask_loc.shape[0]
    chan = z_in.shape[2] if first else z_in.shape[1]
    hid = chan if first else t_in.shape[0]
    wb = min(2 * LANES, width)
    nw = width // wb
    specs, out_specs = local_specs(chan, hid, n_dev, wb, nw, chunk, first, last)
    args = [z_in] + ([] if first else [t_in]) + ([] if last else [mask_loc])
    n_blocked = len(args)
    wts = list(prev or ()) + list(nxt or ())
    args += wts
    specs += [pl.BlockSpec(memory_space=pltpu.VMEM)] * len(wts)
    alias = {}
    if last:
        alias = {len(args): 0}
        args.append(out_full)
        specs.append(pl.BlockSpec(memory_space=pl.ANY))
        out_shape = [jax.ShapeDtypeStruct(out_full.shape, BF16)]
    else:
        out_shape = [
            jax.ShapeDtypeStruct((rows_loc, chan, width), BF16),
            jax.ShapeDtypeStruct((n_dev, 2 * hid // n_dev, rows_loc, width), BF16),
        ]

    def body(*refs):
        w_refs = refs[n_blocked : n_blocked + len(wts)]
        n_prev = len(prev or ())
        outs = refs[len(args) : len(args) + len(out_shape)]
        finish_and_project(refs[:n_blocked] + outs, (w_refs[:n_prev], w_refs[n_prev:]), refs[-2:], first, last)

    return pl.pallas_call(
        body,
        grid=(rows_loc // ROWS, nw),
        in_specs=specs,
        out_specs=out_specs,
        out_shape=out_shape,
        scratch_shapes=local_scratch(hid, wb),
        input_output_aliases=alias,
        compiler_params=pltpu.CompilerParams(vmem_limit_bytes=60 * 2**20),
        name=f"local_{chunk}",
    )(*args)


def out_kernel(*refs, chunks):
    t_ref = refs[-1]
    total = None
    for p in range(chunks):
        a_val = refs[p][...].reshape(-1, refs[p].shape[-1])
        b_val = refs[chunks + p][...].reshape(-1, refs[chunks + p].shape[-1])
        part = lax.dot_general(a_val, b_val, (((1,), (1,)), ((), ())), preferred_element_type=F32)
        total = part if total is None else total + part
    t_ref[...] = total.astype(BF16).reshape(t_ref.shape)


def in_kernel(*refs, chunks):
    b_ref, t_ref = refs[chunks], refs[-1]
    b_val = b_ref[...].reshape(-1, b_ref.shape[-1])
    n_dev, _, rows, _ = t_ref.shape
    share = n_dev // chunks
    for p in range(chunks):
        a_val = refs[p][...].reshape(-1, refs[p].shape[-1])
        part = lax.dot_general(a_val, b_val, (((0,), (0,)), ((), ())), preferred_element_type=F32)
        t_ref[p * share : (p + 1) * share] = part.astype(BF16).reshape(share, 1, rows, t_ref.shape[-1])


def offsets(nx, ny):
    signed = lambda n: [d if d <= n // 2 else d - n for d in range(n)]
    classes = {}
    for dx in signed(nx):
        for dy in signed(ny):
            if dx or dy:
                lo, hi = sorted((abs(dx), abs(dy)))
                classes.setdefault((lo != hi, lo, hi), []).append((dx, dy))
    return [sorted(classes[key], key=lambda o: (o[0] * o[1] < 0, o)) for key in sorted(classes)]


def start_exchange(src, dst, send_sem, recv_sem, self_sem, nx, ny, pieces):
    row, col = lax.axis_index("dap2"), lax.axis_index("dap")
    n_col = 2 * nx
    me = row * n_col + col
    chip, core = col // 2, lax.rem(col, 2)
    step = src.shape[1] // pieces

    def send(dx, dy, other, start, size):
        to_row = lax.rem(row + dy % ny, ny)
        to_col = lax.rem(chip + dx % nx, nx) * 2 + lax.rem(core + other, 2)
        pltpu.make_async_remote_copy(
            src_ref=src.at[to_row * n_col + to_col, pl.ds(start, size)],
            dst_ref=dst.at[me, pl.ds(start, size)],
            send_sem=send_sem,
            recv_sem=recv_sem,
            device_id={"dap2": to_row, "dap": to_col},
            device_id_type=pl.DeviceIdType.MESH,
        ).start()

    send(0, 0, 1, 0, src.shape[1])
    pltpu.make_async_copy(src.at[me], dst.at[me], self_sem).start()
    for group in offsets(nx, ny):

        def piece(h, carry):
            for other in range(2):
                for dx, dy in group:
                    send(dx, dy, other, h * step, step)
            return carry

        lax.fori_loop(0, pieces, piece, 0)


def wait_received(dst, recv_sem, self_sem):
    others = dst.at[pl.ds(0, dst.shape[0] - 1)]
    pltpu.make_async_copy(others, others, recv_sem).wait()
    pltpu.make_async_copy(dst.at[0], dst.at[0], self_sem).wait()


def wait_sent(src, send_sem):
    others = src.at[pl.ds(0, src.shape[0] - 1)]
    pltpu.make_async_copy(others, others, send_sem).wait()


def tri_specs(n_dev, per, rows, width, q, outgoing):
    a_spec = pl.BlockSpec((n_dev, 1, rows, width), lambda c: (0, c, 0, 0))
    if outgoing:
        b_specs = [pl.BlockSpec((n_dev // CHUNKS, 1, rows, width), lambda c: (q, per + c, 0, 0))] * CHUNKS
    else:
        b_specs = [pl.BlockSpec((n_dev, 1, rows, width), lambda c: (0, per + c, 0, 0))]
    return [a_spec] * CHUNKS + b_specs, [a_spec]


def update_call(ab0, z_cur, t_prev, mask_loc, prev, here, done, nxt, outgoing, first, last, mesh, cid):
    ny, nx = mesh.shape["dap2"], mesh.shape["dap"] // 2
    n_dev, per2, rows_loc, width = ab0.shape
    per = per2 // 2
    z0 = z_cur[0]
    chan, hid = z0.shape[1], per * n_dev
    wb = min(2 * LANES, width)
    nw = width // wb
    grid = (rows_loc // ROWS, nw)
    hbm = [ab0, z0, z_cur[1], mask_loc] + ([] if first else [t_prev])
    wts = list(prev or ()) + list(here) + list(done) + list(nxt or ())
    cuts = [len(prev or ()), len(here), len(done), len(nxt or ())]
    ab_type = jax.ShapeDtypeStruct(ab0.shape, BF16)
    t_type = jax.ShapeDtypeStruct((n_dev, per, rows_loc, width), BF16)
    z_type = jax.ShapeDtypeStruct((rows_loc, chan, width), BF16)
    out_type = jax.ShapeDtypeStruct((rows_loc, mask_loc.shape[1], chan), BF16)
    out_shape = [ab_type] * 3 + [t_type] * 4 + [z_type] + ([out_type] if last else [z_type, ab_type])

    def body(*refs):
        ins, w_refs = refs[: len(hbm)], refs[len(hbm) : len(hbm) + len(wts)]
        outs = refs[len(hbm) + len(wts) : len(hbm) + len(wts) + len(out_shape)]
        t_scr, ab_scr, send_sem, recv_sem, self_sem = refs[-5:]
        groups, at = [], 0
        for cut in cuts:
            groups.append(w_refs[at : at + cut])
            at += cut
        ab0_ref, z0_ref, z1_ref, mask_ref = ins[:4]
        ab1_ref, got0, got1, t0_ref, t1_ref, back0, back1, z1_out = outs[:8]
        scr = (t_scr, ab_scr)
        row, col = lax.axis_index("dap2"), lax.axis_index("dap")
        barrier = pltpu.get_barrier_semaphore()
        for k in range(1, n_dev):
            peer = {"dap2": lax.rem(row + k // (2 * nx), ny), "dap": lax.rem(col + k % (2 * nx), 2 * nx)}
            pl.semaphore_signal(barrier, inc=1, device_id=peer, device_id_type=pl.DeviceIdType.MESH)
        pl.semaphore_wait(barrier, n_dev - 1)

        def go(n, src, dst):
            start_exchange(src, dst, send_sem.at[n], recv_sem.at[n], self_sem.at[n], nx, ny, PIECES)

        def local(chunk, w_sets, fst, lst, *arrays):
            specs, out_specs = local_specs(chan, hid, n_dev, wb, nw, chunk, fst, lst)
            pltpu.emit_pipeline(
                lambda *blocks: finish_and_project(blocks, w_sets, scr, fst, lst),
                grid=grid,
                in_specs=specs,
                out_specs=out_specs,
            )(*arrays)

        def tri(q, t_ref):
            specs, out_specs = tri_specs(n_dev, per, rows_loc, width, q, outgoing)
            kernel = out_kernel if outgoing else in_kernel
            b_refs = [got0, got1] if outgoing else [(got0, got1)[q]]
            pltpu.emit_pipeline(
                lambda *blocks: kernel(*blocks, chunks=CHUNKS), grid=(per,), in_specs=specs, out_specs=out_specs
            )(got0, got1, *b_refs, t_ref)

        def rows_of(ref):
            return ref.reshape(hid, rows_loc, width)

        go(0, ab0_ref, got0)
        if first:
            local(1, (None, groups[1]), True, False, z1_ref, mask_ref, z1_out, ab1_ref)
        else:
            local(1, (groups[0], groups[1]), False, False, z1_ref, ins[4], mask_ref, z1_out, ab1_ref)
        go(1, ab1_ref, got1)
        wait_received(got0, recv_sem.at[0], self_sem.at[0])
        wait_received(got1, recv_sem.at[1], self_sem.at[1])
        tri(0, t0_ref)
        go(2, t0_ref, back0)
        tri(1, t1_ref)
        go(3, t1_ref, back1)
        wait_received(back0, recv_sem.at[2], self_sem.at[2])
        if last:
            local(0, (groups[2], None), False, True, z0_ref, rows_of(back0), outs[8])
        else:
            local(0, (groups[2], groups[3]), False, False, z0_ref, rows_of(back0), mask_ref, outs[8], outs[9])
        wait_received(back1, recv_sem.at[3], self_sem.at[3])
        for n, src in enumerate((ab0_ref, ab1_ref, t0_ref, t1_ref)):
            wait_sent(src, send_sem.at[n])

    res = pl.pallas_call(
        body,
        in_specs=[pl.BlockSpec(memory_space=pltpu.HBM)] * len(hbm) + [pl.BlockSpec(memory_space=pltpu.VMEM)] * len(wts),
        out_specs=[pl.BlockSpec(memory_space=pltpu.HBM)] * len(out_shape),
        out_shape=out_shape,
        scratch_shapes=local_scratch(hid, wb) + [pltpu.SemaphoreType.DMA((4,))] * 3,
        compiler_params=pltpu.CompilerParams(collective_id=cid, has_side_effects=True, vmem_limit_bytes=60 * 2**20),
        name=f"update_{cid}",
    )(*hbm, *wts)
    t1_rows = res[6].reshape(hid, rows_loc, width)
    if last:
        return res[8], res[7], t1_rows
    return res[9], [res[8], res[7]], t1_rows


def solution(mesh):
    n_dev = mesh.shape["dap2"] * mesh.shape["dap"]
    row_spec = P(ALL_ROWS, None, None)
    mask_spec = P(ALL_ROWS, None)

    def local_stack(pair_rep, pair_mask, norm_in, norm_out, w_ab, w_gate, w_out):
        width = pair_rep.shape[1] // CHUNKS
        wb = min(2 * LANES, width)

        def spread(vec):
            return jnp.broadcast_to(vec.astype(F32)[:, None], (vec.shape[0], wb))

        steps = [(layer, upd) for layer in range(w_ab.shape[0]) for upd in range(2)]

        def before(s):
            l, u = steps[s]
            return (spread(norm_in[l, u, 0]), spread(norm_in[l, u, 1]), w_ab[l, u].T)

        def after(s):
            l, u = steps[s]
            gains = tuple(spread(v) for v in (norm_in[l, u, 0], norm_in[l, u, 1], norm_out[l, u, 0], norm_out[l, u, 1]))
            return gains + (w_gate[l, u].T, w_out[l, u].T)

        z_first, ab0 = local_call(pair_rep, None, pair_mask, None, before(0), 0, None, n_dev, width)
        z_cur, t_prev = [z_first, pair_rep], None
        for s, (_, upd) in enumerate(steps):
            first, last = s == 0, s + 1 == len(steps)
            res = update_call(
                ab0, z_cur, t_prev, pair_mask, None if first else after(s - 1), before(s), after(s),
                None if last else before(s + 1), upd == 0, first, last, mesh, 1 + upd + (2 if last else 0) + (4 if first else 0),
            )
            if last:
                out, z_one, t_one = res
                return local_call(z_one, t_one, pair_mask, after(s), None, 1, out, n_dev, width)[0]
            ab0, z_cur, t_prev = res

    def mapped(*args):
        with jax.sharding.use_abstract_mesh(mesh.abstract_mesh):
            return jax.shard_map(local_stack, mesh=mesh, in_specs=(row_spec, mask_spec, P(), P(), P(), P(), P()), out_specs=row_spec, check_vma=False)(*args)

    return mapped
```

time: 2200 us -> 2080 us (0.945); the launches traced: 2200 us -> 2050 us
  Pallas kernels: 724 us -> 2010 us
  waiting for transfers between devices: 726 us -> 0 us
  blocking collectives: 623 us -> 0 us
  starting transfers between devices: 89.2 us -> 0 us
    pallas_call x26 -> x8, Pallas kernels: 724 us -> 2010 us  [the longest x6 1950 us: update_call(): pl.pallas_call(body, in_specs=[pl.BlockSpec(memory_space=pltpu.HBM)] * le...]
    all_to_all x18 -> x0, waiting for transfers between devices: 726 us -> none  [exchange(): lax.all_to_all(flat, ROW_AXES, 0, 0, tiled=True).reshape(blocks.shape)]
    all_to_all x6 -> x0, blocking collectives: 623 us -> none  [exchange(): lax.all_to_all(flat, ROW_AXES, 0, 0, tiled=True).reshape(blocks.shape)]
    all_to_all x18 -> x0, starting transfers between devices: 89.2 us -> none  [exchange(): lax.all_to_all(flat, ROW_AXES, 0, 0, tiled=True).reshape(blocks.shape)]
  transfers between devices with their start and end apart: 18 -> 0, of which waited for: 18 -> 0; matrix products, arithmetic and copies ran while one was open for 1% -> 0% of each run, Pallas kernels for 28% -> 0%
where the time goes in v2:
time: 2080 us; the launch traced here: 2050 us
  Pallas kernels  2010 us (97%)
  local copies, waits for them, and re-layouts  39.9 us (2%)
    pallas_call x6, Pallas kernels, update_call(): pl.pallas_call(body, in_specs=[pl.BlockSpec(memory_space=pltpu.HBM)] * le...  1950 us
    pallas_call x2, Pallas kernels, local_call(): pl.pallas_call(body, grid=(rows_loc // ROWS, nw), in_specs=specs, out_spe...  61.9 us

profile of v2, /device:TPU:103, one launch (start us, length us, event | category | flops | bytes accessed | tf_op | source)
XLA Modules:
  0.0 2055.0 jit_solution(3691680074805621843)
XLA Ops:
  0.0 0.8 bitcast_convert_fusion.2
  0.8 0.7 broadcast_in_dim.48.refs_2_.refs_4_.refs_7_.refs_5_
  1.5 0.7 broadcast_in_dim.49.refs_3_.refs_5_.refs_8_.refs_6_
  2.3 1.3 fusion
  3.5 0.8 copy.27
  4.3 0.0 copy-start.2
  4.3 0.0 copy-start
  4.3 0.0 copy-start.1
  4.3 33.3 %local_0.1 = (bf16[32,128,512]{2,1,0:T(8,128)(2,1)}, bf16[32,8,32,512]{3,2,1,0:T(8,128)(2,1)}) custom-call(bf16[32,1024,128]{2,1,0:T(8,128)(2,1)} %refs_2_.1, s32[32,1024]{1,0:T(8,128)} %refs_3_.11, f32[128,256]{1,0:T(8,128)} %broadcast_in_dim.48.refs_2_.refs_4_.refs_7_.refs_5_, f32[128,256]{1,0:T(8,128)} %broadcast_in_dim.49.refs_3_.refs_5_.refs_8_.refs_6_, ...), custom_call_target="tpu_custom_call" | custom-call | tf_op jit(solution)/shard_map/local_0/pallas_call | solution.py:171
  37.6 0.7 broadcast_in_dim.52.refs_13_.refs_11_.refs_14_.refs_5_
  38.4 0.7 broadcast_in_dim.53.refs_14_.refs_12_.refs_15_.refs_6_
  39.1 0.0 copy-done.2
  39.1 0.7 broadcast_in_dim.50.refs_9_.refs_7_
  39.9 0.7 broadcast_in_dim.51.refs_10_.refs_8_
  40.6 0.8 copy.30
  41.4 0.0 copy-done
  41.4 0.7 copy.28
  42.1 0.0 copy-done.1
  42.1 0.7 copy.29
  42.8 323.6 %update_5.1 = (bf16[32,8,32,512]{3,2,1,0:T(8,128)(2,1)}, bf16[32,8,32,512]{3,2,1,0:T(8,128)(2,1)}, bf16[32,8,32,512]{3,2,1,0:T(8,128)(2,1)}, bf16[32,4,32,512]{3...) custom-call(bf16[32,8,32,512]{3,2,1,0:T(8,128)(2,1)} %get-tuple-elem, ...), custom_call_target="tpu_custom_call" | custom-call | tf_op jit(solution)/shard_map/update_5/pallas_call | solution.py:349
  366.5 0.8 broadcast_in_dim.56.refs_20_.refs_11_.refs_14_.refs_5_
  367.2 0.7 broadcast_in_dim.57.refs_21_.refs_12_.refs_15_.refs_6_
  368.0 0.7 broadcast_in_dim.54.refs_16_.refs_7_
  368.7 0.7 broadcast_in_dim.55.refs_17_.refs_8_
  369.5 0.8 copy.33
  370.2 0.7 copy.31
  370.9 0.7 copy.32
  371.6 323.6 %update_2.2 = (bf16[32,8,32,512]{3,2,1,0:T(8,128)(2,1)}, bf16[32,8,32,512]{3,2,1,0:T(8,128)(2,1)}, bf16[32,8,32,512]{3,2,1,0:T(8,128)(2,1)}, bf16[32,4,32,512]{3...) custom-call(bf16[32,8,32,512]{3,2,1,0:T(8,128)(2,1)} %get-tuple-elem, ...), custom_call_target="tpu_custom_call" | custom-call | tf_op jit(solution)/shard_map/update_2/pallas_call | solution.py:349
  695.2 0.7 broadcast_in_dim.60.refs_20_.refs_11_.refs_14_.refs_5_
  695.9 0.7 broadcast_in_dim.61.refs_21_.refs_12_.refs_15_.refs_6_
  696.7 0.7 broadcast_in_dim.58.refs_16_.refs_7_
  697.4 0.7 broadcast_in_dim.59.refs_17_.refs_8_
  698.2 0.8 copy.36
  698.9 0.7 copy.34
  699.6 0.7 copy.35
  700.4 325.3 %update_1.2 = (bf16[32,8,32,512]{3,2,1,0:T(8,128)(2,1)}, bf16[32,8,32,512]{3,2,1,0:T(8,128)(2,1)}, bf16[32,8,32,512]{3,2,1,0:T(8,128)(2,1)}, bf16[32,4,32,512]{3...) custom-call(bf16[32,8,32,512]{3,2,1,0:T(8,128)(2,1)} %get-tuple-elem, ...), custom_call_target="tpu_custom_call" | custom-call | tf_op jit(solution)/shard_map/update_1/pallas_call | solution.py:349
  1025.7 0.7 broadcast_in_dim.64.refs_20_.refs_11_.refs_14_.refs_5_
  1026.4 0.7 broadcast_in_dim.65.refs_21_.refs_12_.refs_15_.refs_6_
  1027.1 0.7 broadcast_in_dim.62.refs_16_.refs_7_
  1027.9 0.7 broadcast_in_dim.63.refs_17_.refs_8_
  1028.6 0.8 copy.39
  1029.4 0.7 copy.37
  1030.1 0.7 copy.38
  1030.8 317.2 %update_2.3 = (bf16[32,8,32,512]{3,2,1,0:T(8,128)(2,1)}, bf16[32,8,32,512]{3,2,1,0:T(8,128)(2,1)}, bf16[32,8,32,512]{3,2,1,0:T(8,128)(2,1)}, bf16[32,4,32,512]{3...) custom-call(bf16[32,8,32,512]{3,2,1,0:T(8,128)(2,1)} %get-tuple-elem, ...), custom_call_target="tpu_custom_call" | custom-call | tf_op jit(solution)/shard_map/update_2/pallas_call | solution.py:349
  1348.0 0.8 broadcast_in_dim.68.refs_20_.refs_11_.refs_14_.refs_2_
  1348.8 0.7 broadcast_in_dim.69.refs_21_.refs_12_.refs_15_.refs_3_
  1349.5 0.7 broadcast_in_dim.66.refs_16_.refs_7_
  1350.2 0.7 broadcast_in_dim.67.refs_17_.refs_8_
  1351.0 0.8 copy.42
  1351.7 0.7 copy.40
  1352.5 0.7 copy.41
  1353.2 344.4 %update_1.3 = (bf16[32,8,32,512]{3,2,1,0:T(8,128)(2,1)}, bf16[32,8,32,512]{3,2,1,0:T(8,128)(2,1)}, bf16[32,8,32,512]{3,2,1,0:T(8,128)(2,1)}, bf16[32,4,32,512]{3...) custom-call(bf16[32,8,32,512]{3,2,1,0:T(8,128)(2,1)} %get-tuple-elem, ...), custom_call_target="tpu_custom_call" | custom-call | tf_op jit(solution)/shard_map/update_1/pallas_call | solution.py:349
  1697.5 0.7 broadcast_in_dim.70.refs_16_.refs_4_
  1698.3 0.7 broadcast_in_dim.71.refs_17_.refs_5_
  1699.0 0.7 copy.43
  1699.7 0.7 copy.44
  1700.5 317.8 %update_4.1 = (bf16[32,8,32,512]{3,2,1,0:T(8,128)(2,1)}, bf16[32,8,32,512]{3,2,1,0:T(8,128)(2,1)}, bf16[32,8,32,512]{3,2,1,0:T(8,128)(2,1)}, bf16[32,4,32,512]{3...) custom-call(bf16[32,8,32,512]{3,2,1,0:T(8,128)(2,1)} %get-tuple-elem, ...), custom_call_target="tpu_custom_call" | custom-call | tf_op jit(solution)/shard_map/update_4/pallas_call | solution.py:349
  2018.3 28.6 %local_1.1 = bf16[32,1024,128]{2,1,0:T(8,128)(2,1)} custom-call(bf16[32,128,512]{2,1,0:T(8,128)(2,1)} %get-tuple-element.52.refs_0_, bf16[128,32,512]{2,1,0:T(8,128)(2,1)} %bitcast.132, f32[128,256]{1,0:T(8,128)} %broadcast_in_dim.68.refs_20_.refs_11_.refs_14_.refs_2_, ...), custom_call_target="tpu_custom_call", output_to_operand_aliasing={{}: (8, {})} | custom-call | tf_op jit(solution)/shard_map/local_1/pallas_call | solution.py:171
  2046.9 7.7 copy.47
  (3 shorter events, 0.0 us)
Async XLA Ops:
  4.3 34.8 %copy-start.2 = (bf16[3,2,2,128]{3,2,1,0:T(2,128)(2,1)S(1)}, bf16[3,2,2,128]{3,2,1,0:T(2,128)(2,1)}, u32[]{:S(2)}) copy-start(bf16[3,2,2,128]{3,2,1,0:T(2,128)(2,1)} %param.10) | copy-start | bytes 9220
  4.3 37.1 %copy-start = (bf16[3,2,128,128]{3,2,1,0:T(8,128)(2,1)S(1)}, bf16[3,2,128,128]{3,2,1,0:T(8,128)(2,1)}, u32[]{:S(2)}) copy-start(bf16[3,2,128,128]{3,2,1,0:T(8,128)(2,1)} %param.12) | copy-start | bytes 589828
  4.3 37.8 %copy-start.1 = (bf16[3,2,128,128]{3,2,1,0:T(8,128)(2,1)S(1)}, bf16[3,2,128,128]{3,2,1,0:T(8,128)(2,1)}, u32[]{:S(2)}) copy-start(bf16[3,2,128,128]{3,2,1,0:T(8,128)(2,1)} %param.13) | copy-start | bytes 589828

commit v3 on v2

--- a/solution.py
+++ b/solution.py
@@ -25,7 +25,7 @@
 
 
 def sigmoid(values):
-    return 1.0 / (1.0 + jnp.exp(-values))
+    return 0.5 * jnp.tanh(0.5 * values) + 0.5
 
 
 def finish_and_project(refs, wts, scr, first, last):
@@ -100,7 +100,7 @@
                 ab_scr[blk, pl.ds(start, hid), :] = val[:, blk * LANES : (blk + 1) * LANES]
         return carry
 
-    lax.fori_loop(0, rows, one_row, 0)
+    lax.fori_loop(0, rows, one_row, 0, unroll=4)
 
     if not last:
         dests, per_dest = ab_out.shape[0], ab_out.shape[1] // 2

time: 2080 us -> 2010 us (0.966)
  Pallas kernels: 2010 us -> 1950 us
    pallas_call x6, Pallas kernels: 1950 us -> 1920 us  [update_call(): pl.pallas_call(body, in_specs=[pl.BlockSpec(memory_space=pltpu.HBM)] * le...]
    pallas_call x2, Pallas kernels: 61.9 us -> 34.4 us  [local_call(): pl.pallas_call(body, grid=(rows_loc // ROWS, nw), in_specs=specs, out_spe...]
where the time goes in v3:
time: 2010 us; the launch traced here: 1990 us
  Pallas kernels  1950 us (97%)
  local copies, waits for them, and re-layouts  39.9 us (2%)
    pallas_call x6, Pallas kernels, update_call(): pl.pallas_call(body, in_specs=[pl.BlockSpec(memory_space=pltpu.HBM)] * le...  1920 us

profile of v3, /device:TPU:103, one launch (start us, length us, event | category | flops | bytes accessed | tf_op | source)
XLA Modules:
  0.0 1994.2 jit_solution(6949389282027431279)
XLA Ops:
  0.0 0.8 bitcast_convert_fusion.2
  0.8 0.7 broadcast_in_dim.48.refs_2_.refs_4_.refs_7_.refs_5_
  1.5 0.7 broadcast_in_dim.49.refs_3_.refs_5_.refs_8_.refs_6_
  2.3 1.3 fusion
  3.5 0.8 copy.27
  4.3 0.0 copy-start.2
  4.3 0.0 copy-start
  4.3 0.0 copy-start.1
  4.3 17.8 local_0.1
  22.1 0.7 broadcast_in_dim.52.refs_13_.refs_11_.refs_14_.refs_5_
  22.9 0.7 broadcast_in_dim.53.refs_14_.refs_12_.refs_15_.refs_6_
  23.6 0.0 copy-done.2
  23.6 0.7 broadcast_in_dim.50.refs_9_.refs_7_
  24.4 0.7 broadcast_in_dim.51.refs_10_.refs_8_
  25.1 0.8 copy.30
  25.9 0.0 copy-done
  25.9 0.7 copy.28
  26.6 0.0 copy-done.1
  26.6 0.7 copy.29
  27.4 319.6 %update_5.1 = (bf16[32,8,32,512]{3,2,1,0:T(8,128)(2,1)}, bf16[32,8,32,512]{3,2,1,0:T(8,128)(2,1)}, bf16[32,8,32,512]{3,2,1,0:T(8,128)(2,1)}, bf16[32,4,32,512]{3...) custom-call(bf16[32,8,32,512]{3,2,1,0:T(8,128)(2,1)} %get-tuple-elem, ...), custom_call_target="tpu_custom_call" | custom-call | tf_op jit(solution)/shard_map/update_5/pallas_call | solution.py:349
  346.9 0.8 broadcast_in_dim.56.refs_20_.refs_11_.refs_14_.refs_5_
  347.7 0.7 broadcast_in_dim.57.refs_21_.refs_12_.refs_15_.refs_6_
  348.4 0.7 broadcast_in_dim.54.refs_16_.refs_7_
  349.2 0.7 broadcast_in_dim.55.refs_17_.refs_8_
  349.9 0.8 copy.33
  350.7 0.7 copy.31
  351.4 0.7 copy.32
  352.1 322.1 %update_2.2 = (bf16[32,8,32,512]{3,2,1,0:T(8,128)(2,1)}, bf16[32,8,32,512]{3,2,1,0:T(8,128)(2,1)}, bf16[32,8,32,512]{3,2,1,0:T(8,128)(2,1)}, bf16[32,4,32,512]{3...) custom-call(bf16[32,8,32,512]{3,2,1,0:T(8,128)(2,1)} %get-tuple-elem, ...), custom_call_target="tpu_custom_call" | custom-call | tf_op jit(solution)/shard_map/update_2/pallas_call | solution.py:349
  674.2 0.7 broadcast_in_dim.60.refs_20_.refs_11_.refs_14_.refs_5_
  674.9 0.7 broadcast_in_dim.61.refs_21_.refs_12_.refs_15_.refs_6_
  675.6 0.7 broadcast_in_dim.58.refs_16_.refs_7_
  676.4 0.7 broadcast_in_dim.59.refs_17_.refs_8_
  677.1 0.8 copy.36
  677.9 0.7 copy.34
  678.6 0.7 copy.35
  679.3 319.1 %update_1.2 = (bf16[32,8,32,512]{3,2,1,0:T(8,128)(2,1)}, bf16[32,8,32,512]{3,2,1,0:T(8,128)(2,1)}, bf16[32,8,32,512]{3,2,1,0:T(8,128)(2,1)}, bf16[32,4,32,512]{3...) custom-call(bf16[32,8,32,512]{3,2,1,0:T(8,128)(2,1)} %get-tuple-elem, ...), custom_call_target="tpu_custom_call" | custom-call | tf_op jit(solution)/shard_map/update_1/pallas_call | solution.py:349
  998.4 0.7 broadcast_in_dim.64.refs_20_.refs_11_.refs_14_.refs_5_
  999.2 0.7 broadcast_in_dim.65.refs_21_.refs_12_.refs_15_.refs_6_
  999.9 0.7 broadcast_in_dim.62.refs_16_.refs_7_
  1000.6 0.7 broadcast_in_dim.63.refs_17_.refs_8_
  1001.4 0.8 copy.39
  1002.1 0.7 copy.37
  1002.9 0.7 copy.38
  1003.6 313.2 %update_2.3 = (bf16[32,8,32,512]{3,2,1,0:T(8,128)(2,1)}, bf16[32,8,32,512]{3,2,1,0:T(8,128)(2,1)}, bf16[32,8,32,512]{3,2,1,0:T(8,128)(2,1)}, bf16[32,4,32,512]{3...) custom-call(bf16[32,8,32,512]{3,2,1,0:T(8,128)(2,1)} %get-tuple-elem, ...), custom_call_target="tpu_custom_call" | custom-call | tf_op jit(solution)/shard_map/update_2/pallas_call | solution.py:349
  1316.8 0.8 broadcast_in_dim.68.refs_20_.refs_11_.refs_14_.refs_2_
  1317.5 0.7 broadcast_in_dim.69.refs_21_.refs_12_.refs_15_.refs_3_
  1318.3 0.7 broadcast_in_dim.66.refs_16_.refs_7_
  1319.0 0.7 broadcast_in_dim.67.refs_17_.refs_8_
  1319.8 0.8 copy.42
  1320.5 0.7 copy.40
  1321.2 0.7 copy.41
  1322.0 328.0 %update_1.3 = (bf16[32,8,32,512]{3,2,1,0:T(8,128)(2,1)}, bf16[32,8,32,512]{3,2,1,0:T(8,128)(2,1)}, bf16[32,8,32,512]{3,2,1,0:T(8,128)(2,1)}, bf16[32,4,32,512]{3...) custom-call(bf16[32,8,32,512]{3,2,1,0:T(8,128)(2,1)} %get-tuple-elem, ...), custom_call_target="tpu_custom_call" | custom-call | tf_op jit(solution)/shard_map/update_1/pallas_call | solution.py:349
  1650.0 0.7 broadcast_in_dim.70.refs_16_.refs_4_
  1650.8 0.7 broadcast_in_dim.71.refs_17_.refs_5_
  1651.5 0.7 copy.43
  1652.2 0.7 copy.44
  1652.9 316.6 %update_4.1 = (bf16[32,8,32,512]{3,2,1,0:T(8,128)(2,1)}, bf16[32,8,32,512]{3,2,1,0:T(8,128)(2,1)}, bf16[32,8,32,512]{3,2,1,0:T(8,128)(2,1)}, bf16[32,4,32,512]{3...) custom-call(bf16[32,8,32,512]{3,2,1,0:T(8,128)(2,1)} %get-tuple-elem, ...), custom_call_target="tpu_custom_call" | custom-call | tf_op jit(solution)/shard_map/update_4/pallas_call | solution.py:349
  1969.5 16.6 local_1.1
  1986.1 7.7 copy.47
  (3 shorter events, 0.0 us)
Async XLA Ops:
  4.3 19.3 copy-start.2
  4.3 21.6 %copy-start = (bf16[3,2,128,128]{3,2,1,0:T(8,128)(2,1)S(1)}, bf16[3,2,128,128]{3,2,1,0:T(8,128)(2,1)}, u32[]{:S(2)}) copy-start(bf16[3,2,128,128]{3,2,1,0:T(8,128)(2,1)} %param.12) | copy-start | bytes 589828
  4.3 22.3 %copy-start.1 = (bf16[3,2,128,128]{3,2,1,0:T(8,128)(2,1)S(1)}, bf16[3,2,128,128]{3,2,1,0:T(8,128)(2,1)}, u32[]{:S(2)}) copy-start(bf16[3,2,128,128]{3,2,1,0:T(8,128)(2,1)} %param.13) | copy-start | bytes 589828
